TPU v7x, 128 devices: a whole 4x4x4 slice. The times are simulated.
128 devices in a mesh: head: 32 (over z, y, x_hi), kdim: 4 (over x_lo, core).
Axes of the slice: x: 4 (x_hi: 2, x_lo: 2; x = x_hi * 2 + x_lo), y: 4, z: 4, core: 2. Of those that a mesh axis runs over, the one named last changes fastest.
Arguments:
- hidden: bfloat16 [3, 1024, 8192], P(None, None, 'kdim'), may hold values from -6 to 6
- joined_weight: bfloat16 [3, 8192, 10240], P(None, 'kdim', 'head'), may hold values from -0.0625 to 0.0625
- src_block: int32 [8], replicated, may hold values from 0 to 7, each once
- group_map: int32 [8], replicated, may hold values from 0 to 7, each once
- q_slot: int32 [64], replicated, may hold values from 0 to 7, as said below
Outputs:
- qkv: float32 [3, 1024, 16384], P(None, 'kdim', 'head')
Inputs may be any that keep to these rules, and one draw needn't show every extreme that they name: `q_slot`: for every key head g, the entries g * 8 to g * 8 + 7 are a permutation of 0 to 7.
All inputs are finite; a program needn't handle non-finite values.
Results may differ from a plain program's by a relative error of at most 0.0003.
Values may be sent and summed in bfloat16 or wider, within the bound.
No kernel may reach another device: no remote copies, remote signals or barrier semaphores. Data moves between devices by JAX's collectives and lax.ppermute only.
A program may use at most 64 MiB of HBM per device.

v0:
```python
import jax
import jax.numpy as jnp
from jax import lax
from jax.sharding import PartitionSpec as P

HEAD_DIM = 128
Q_HEADS = 64
KV_HEADS = 8
GROUP = 8
BLOCK = 1280


def cut_along(x, dim, size):
    before, after = (x.shape[:dim], x.shape[dim + 1 :])
    return jnp.moveaxis(x.reshape(*before, size, -1, *after), dim, 0)


def sent_and_summed(x, axis, dim):
    size = lax.axis_size(axis)
    blocks = lax.all_to_all(cut_along(x, dim, size), axis, 0, 0, tiled=True)
    return jnp.sum(blocks, axis=0)


def column_table(src_block, group_map, q_slot, head_count):
    group_devs = head_count // KV_HEADS
    slot_count = Q_HEADS // head_count
    devices = jnp.arange(head_count, dtype=jnp.int32)
    group_ids = devices // group_devs
    quarter = devices % group_devs
    rank_ids = jnp.arange(KV_HEADS, dtype=jnp.int32)
    owner = jnp.sum(rank_ids[None, :] * (group_map[None, :] == group_ids[:, None]), axis=1)
    block_start = (
        jnp.sum(src_block[None, :] * (rank_ids[None, :] == owner[:, None]), axis=1) * BLOCK
    )
    members = owner[:, None] * GROUP + jnp.arange(GROUP, dtype=jnp.int32)[None, :]
    member_slot = q_slot[members]
    positions = quarter[:, None] * slot_count + jnp.arange(slot_count, dtype=jnp.int32)[None, :]
    local_head = jnp.sum(
        jnp.arange(GROUP, dtype=jnp.int32)[None, None, :]
        * (member_slot[:, None, :] == positions[:, :, None]),
        axis=2,
    )
    q_cols = (
        block_start[:, None, None]
        + local_head[:, :, None] * HEAD_DIM
        + jnp.arange(HEAD_DIM, dtype=jnp.int32)[None, None, :]
    )
    kv_cols = (
        block_start[:, None] + GROUP * HEAD_DIM + jnp.arange(2 * HEAD_DIM, dtype=jnp.int32)[None, :]
    )
    columns = jnp.concatenate([q_cols.reshape(head_count, slot_count * HEAD_DIM), kv_cols], axis=1)
    return columns.reshape(-1)


def pick_blocks(source_rows, table):
    row_count, width = source_rows.shape
    block_count = width // HEAD_DIM
    blocks = source_rows.reshape(row_count, block_count, HEAD_DIM)
    wanted = table.reshape(-1, HEAD_DIM)[:, 0] // HEAD_DIM
    selector = (wanted[:, None] == jnp.arange(block_count, dtype=jnp.int32)[None, :]).astype(
        source_rows.dtype
    )
    picked = jnp.einsum(
        "kb,rbh->rkh",
        selector,
        blocks,
        preferred_element_type=jnp.float32,
        precision=lax.Precision.HIGHEST,
    )
    return picked.reshape(row_count, -1)


def route_direct(payload, table, spread, settle):
    layers, rows, width = payload.shape
    flat = payload.reshape(layers * rows, width)
    spread_rows = spread(flat)
    picked = pick_blocks(spread_rows, table)
    settled = settle(picked)
    return settled.reshape(layers, rows, -1)


def on_device(hidden, joined_weight, src_block, group_map, q_slot):
    head_count = lax.axis_size("head")
    partial_value = jnp.einsum(
        "lrd,ldc->lrc", hidden, joined_weight, preferred_element_type=jnp.float32
    )
    summed = sent_and_summed(partial_value, "kdim", 1)
    table = column_table(src_block, group_map, q_slot, head_count)
    return route_direct(
        summed,
        table,
        lambda piece: lax.all_to_all(piece, "head", split_axis=0, concat_axis=1, tiled=True),
        lambda piece: lax.all_to_all(piece, "head", split_axis=1, concat_axis=0, tiled=True),
    )


def solution(mesh):
    return jax.shard_map(
        on_device,
        mesh=mesh,
        in_specs=(P(None, None, "kdim"), P(None, "kdim", "head"), P(), P(), P()),
        out_specs=P(None, "kdim", "head"),
        check_vma=False,
    )
```

profile of v0, /device:TPU:0, one launch (start us, length us, event | category | flops | bytes accessed | tf_op | source)
XLA Modules:
  0.0 134.1 jit_solution(17637082087116559954)
XLA Ops:
  0.0 11.9 %fusion.7 = f32[3,1024,320]{1,2,0:T(8,128)} fusion(bf16[3,1024,2048]{2,1,0:T(8,128)(2,1)} %param.5, bf16[3,2048,320]{1,2,0:T(8,128)(2,1)} %param.6), kind=kOutput, calls=%fused_computation.35 | convolution fusion | flops 4026531840 | bytes 20447232 | tf_op jit(solution)/shard_map/lrd,ldc->lrc/dot_general | solution.py:84
  11.9 4.4 %copy.30 = f32[3,40,4,8,256]{4,3,1,0,2:T(8,128)} copy(f32[3,40,4,8,256]{4,3,2,1,0:T(8,128)} %bitcast.30) | data formatting | bytes 7864320 | tf_op jit(solution)/shard_map/reshape | solution.py:15
  16.3 4.9 %all-to-all-start = ((f32[4,3,256,320]{2,3,1,0:T(8,128)}), f32[4,3,256,320]{2,3,1,0:T(8,128)}, u32[]{:S(2)}, u32[]{:S(2)}) async-start(f32[4,3,256,320]{2,3,1,0:T(8,128)} %bitcast.27), calls=%async_computation | async-start | bytes 7864320 | tf_op jit(solution)/shard_map/all_to_all | solution.py:20
  21.2 0.1 select_reduce_fusion.2
  21.4 0.1 reshape.150
  21.5 0.1 select_reduce_fusion.1
  21.6 45.0 %all-to-all-done = f32[4,3,256,320]{2,3,1,0:T(8,128)} async-done(((f32[4,3,256,320]{2,3,1,0:T(8,128)}), f32[4,3,256,320]{2,3,1,0:T(8,128)}, u32[]{:S(2)}, u32[]{:S(2)}) %all-to-all-start) | async-done | bytes 3932192 | tf_op jit(solution)/shard_map/all_to_all | solution.py:20
  66.6 2.5 %reduce_sum.36 = f32[3,256,320]{1,2,0:T(8,128)S(1)} reduce(f32[4,3,256,320]{2,3,1,0:T(8,128)} %all-to-all-done, f32[]{:T(128)} %constant.48.clone.1), dimensions={0}, to_apply=%region_0.0 | reduce | flops 737280 | bytes 4915204 | tf_op jit(solution)/shard_map/reduce_sum | solution.py:21
  69.1 1.4 %copy.19 = f32[3,256,320]{2,1,0:T(8,128)} copy(f32[3,256,320]{1,2,0:T(8,128)S(1)} %reduce_sum.36) | data formatting | bytes 1966080 | tf_op jit(solution)/shard_map/reduce_sum | solution.py:21
  70.5 10.9 %all-to-all-start.1 = ((f32[32,24,320]{2,1,0:T(8,128)}), f32[32,24,320]{2,1,0:T(8,128)S(1)}, u32[]{:S(2)}, u32[]{:S(2)}) async-start(f32[32,24,320]{2,1,0:T(8,128)} %bitcast.1), calls=%async_computation.1 | async-start | bytes 2359296 | tf_op jit(solution)/shard_map/all_to_all | solution.py:92
  81.5 1.9 %gather_fusion = s32[256]{0:T(256)S(1)} fusion(s32[64]{0:T(128)S(1)} %copy-done, s32[1024]{0:T(1024)S(1)} %pad_clamp_fusion), kind=kCustom, calls=%fused_computation | custom fusion | bytes 3072 | tf_op jit(solution)/shard_map/gather | solution.py:36
  83.3 0.1 reshape.149
  83.5 0.1 copy.22
  83.6 0.1 add.132
  83.8 0.1 fusion.1
  83.9 17.9 %all-to-all-done.1 = f32[32,24,320]{2,1,0:T(8,128)S(1)} async-done(((f32[32,24,320]{2,1,0:T(8,128)}), f32[32,24,320]{2,1,0:T(8,128)S(1)}, u32[]{:S(2)}, u32[]{:S(2)}) %all-to-all-start.1) | async-done | bytes 983072 | tf_op jit(solution)/shard_map/all_to_all | solution.py:92
  101.9 0.2 copy.20
  102.1 0.6 reshape.146
  102.7 1.4 %convolution_bitcast_fusion = f32[24,128,128]{1,2,0:T(8,128)S(1)} fusion(f32[24,80,128]{2,1,0:T(8,128)S(1)} %reshape.146, s32[128]{0:T(128)S(1)} %fusion.1), kind=kOutput, calls=%fused_computation.2 | convolution fusion | flops 377497600 | bytes 2556416 | tf_op jit(solution)/shard_map/kb,rbh->rkh/dot_general | solution.py:63
  104.1 0.5 copy.23
  104.6 0.2 all_to_all.31
  104.8 0.9 copy.24
  105.8 27.2 %all_to_all.37 = f32[24,32,512]{2,0,1:T(8,128)S(1)} all-to-all(f32[24,32,512]{2,0,1:T(8,128)S(1)} %copy.24), channel_id=1, replica_groups=mesh['head'=32,'kdim'=4] {'head'}, dimensions={1} | all-to-all | bytes 3145728 | tf_op jit(solution)/shard_map/all_to_all | solution.py:93
  133.0 1.1 copy.32
  (20 shorter events, 0.3 us)
Async XLA Ops:
  0.0 81.4 %copy-start = (s32[64]{0:T(128)S(1)}, s32[64]{0:T(128)}, u32[]{:S(2)}) copy-start(s32[64]{0:T(128)} %param.9) | copy-start | bytes 772
  16.3 5.0 %copy-start.1 = (s32[8]{0:T(128)S(1)}, s32[8]{0:T(128)}, u32[]{:S(2)}) copy-start(s32[8]{0:T(128)} %param.8) | copy-start | bytes 100
  16.3 5.2 %copy-start.2 = (s32[8]{0:T(128)S(1)}, s32[8]{0:T(128)}, u32[]{:S(2)}) copy-start(s32[8]{0:T(128)} %param.7) | copy-start | bytes 100
  16.3 50.3 %all-to-all-start = ((f32[4,3,256,320]{2,3,1,0:T(8,128)}), f32[4,3,256,320]{2,3,1,0:T(8,128)}, u32[]{:S(2)}, u32[]{:S(2)}) async-start(f32[4,3,256,320]{2,3,1,0:T(8,128)} %bitcast.27), calls=%async_computation | async-start | bytes 7864320 | tf_op jit(solution)/shard_map/all_to_all | solution.py:20
  70.5 31.4 %all-to-all-start.1 = ((f32[32,24,320]{2,1,0:T(8,128)}), f32[32,24,320]{2,1,0:T(8,128)S(1)}, u32[]{:S(2)}, u32[]{:S(2)}) async-start(f32[32,24,320]{2,1,0:T(8,128)} %bitcast.1), calls=%async_computation.1 | async-start | bytes 2359296 | tf_op jit(solution)/shard_map/all_to_all | solution.py:92
where the time goes:
time: 134 us
  waiting for transfers between devices  62.9 us (47%)
  blocking collectives  27.2 us (20%)
  starting transfers between devices  15.8 us (12%)
  matrix products  13.3 us (10%)
  local copies, waits for them, and re-layouts  11.7 us (9%)
  other arithmetic  3.04 us (2%)
    all_to_all x1, waiting for transfers between devices, sent_and_summed(): blocks = lax.all_to_all(cut_along(x, dim, size), axis, 0, 0, tiled=True)  45 us
    all_to_all x1, blocking collectives, on_device(): lax.all_to_all(piece, 'head', split_axis=1, concat_axis=0, tiled=True)  27.2 us
    all_to_all x1, waiting for transfers between devices, on_device(): lax.all_to_all(piece, 'head', split_axis=0, concat_axis=1, tiled=True)  17.9 us
    dot_general x1, matrix products, on_device(): jnp.einsum('lrd,ldc->lrc', hidden, joined_weight, preferred_element_type=...  11.9 us
    all_to_all x1, starting transfers between devices, on_device(): lax.all_to_all(piece, 'head', split_axis=0, concat_axis=1, tiled=True)  10.9 us
    all_to_all x1, starting transfers between devices, sent_and_summed(): blocks = lax.all_to_all(cut_along(x, dim, size), axis, 0, 0, tiled=True)  4.93 us
    reshape x1, local copies, waits for them, and re-layouts, cut_along(): return jnp.moveaxis(x.reshape(*before, size, -1, *after), dim, 0)  4.39 us
  transfers between devices with their start and end apart: 2, of which 2 were waited for; matrix products, arithmetic and copies ran while one was open for 2% of the time, Pallas kernels for 0%

commit v1 on v0

v1 whole, which is shorter than its diff:
```python
import jax
import jax.numpy as jnp
from jax import lax
from jax.experimental import pallas as pl
from jax.experimental.pallas import tpu as pltpu
from jax.sharding import Mesh, PartitionSpec as P

LAYERS = 3
ROWS = 1024
SLICE = 256
LANES = 128
WIDTH = 320
PADDED = 384
HEADS = 32
GROUP_DEVS = 4
KV_HEADS = 8
GROUP = 8
CODES = 256.0
TOP = 32700.0


def codes_of(amax):
    return jnp.ceil(CODES * jnp.log2(jnp.maximum(amax, 1e-30) * (1.0 / TOP))).astype(jnp.int32)


def scale_of(code):
    return jnp.exp2(code.astype(jnp.float32) * (1.0 / CODES))


def inverse_scale_of(code):
    return jnp.exp2(code.astype(jnp.float32) * (-1.0 / CODES))


def whole(x, inverse):
    return jnp.round(x * inverse).astype(jnp.int32)


def packed(low, high):
    return (low & 0xFFFF) | (high << 16)


def low_of(words):
    return (words << 16) >> 16


def high_of(words):
    return words >> 16


def row_max(*tiles):
    top = jnp.abs(tiles[0])
    for tile in tiles[1:]:
        top = jnp.maximum(top, jnp.abs(tile))
    return jnp.max(top, axis=1, keepdims=True)


def lanes_of(shape):
    return lax.broadcasted_iota(jnp.int32, shape, 1)


def product_kernel(place, hidden, weight, out):
    value = lax.dot_general(
        hidden[0], weight[0], (((1,), (1,)), ((), ())), preferred_element_type=jnp.float32
    )
    odd = place[1]

    @pl.when(odd == 0)
    def _():
        out[0, 0, :, :WIDTH] = value
        out[0, 0, :, WIDTH:] = jnp.zeros((SLICE, PADDED - WIDTH), jnp.float32)

    @pl.when(odd == 1)
    def _():
        out[0, 0, :, :256] = value[:, 64:]
        out[0, 0, :, 256:320] = jnp.zeros((SLICE, 64), jnp.float32)
        out[0, 0, :, 320:] = value[:, :64]


def product(place, hidden, weight, other):
    def token_block(l, x, place):
        core = 1 - place[0] if other else place[0]
        return (l, 2 * x + core, 0)

    return pl.pallas_call(
        product_kernel,
        grid_spec=pltpu.PrefetchScalarGridSpec(
            num_scalar_prefetch=1,
            grid=(LAYERS, 2),
            in_specs=[
                pl.BlockSpec((1, SLICE, 2048), token_block),
                pl.BlockSpec((1, WIDTH, 2048), lambda l, x, place: (l, 0, 0)),
            ],
            out_specs=pl.BlockSpec((1, 1, SLICE, PADDED), lambda l, x, place: (l, x, 0, 0)),
        ),
        out_shape=jax.ShapeDtypeStruct((LAYERS, 2, SLICE, PADDED), jnp.float32),
        cost_estimate=pl.CostEstimate(
            flops=LAYERS * 512 * 2048 * WIDTH * 2, bytes_accessed=12_000_000, transcendentals=0
        ),
        name="product",
    )(place, hidden, weight)


PACK_HEADS = 8


def pack_kernel(place, mine, theirs, out):
    odd = place[1]
    lane = lanes_of((8, LANES))
    spare = (lane >= 64) != (odd == 1)
    slot = lane & 63
    for i in range(PACK_HEADS):
        rows = slice(8 * i, 8 * i + 8)
        rest, codes = [], []
        for l in range(LAYERS):
            tiles = []
            for t in range(3):
                cols = slice(LANES * t, LANES * t + LANES)
                tiles.append(mine[l, 0, rows, cols] + theirs[l, 0, rows, cols])
            code = codes_of(row_max(*tiles))
            inverse = inverse_scale_of(code)
            a, b, c = [whole(tile, inverse) for tile in tiles]
            out[0, i, 8 * l : 8 * l + 8, :] = packed(a, b)
            rest.append(c)
            codes.append(code)
        code = jnp.where(slot == 0, codes[0], jnp.where(slot == 1, codes[1], codes[2]))
        low = rest[0] + pltpu.roll(rest[1], 64, 1)
        high = jnp.where(spare, code, rest[2])
        out[0, i, 24:32, :] = packed(low, high)


def pack(place, mine, theirs):
    block = pl.BlockSpec((LAYERS, 1, 8 * PACK_HEADS, PADDED), lambda x, h, place: (0, x, h, 0))
    return pl.pallas_call(
        pack_kernel,
        grid_spec=pltpu.PrefetchScalarGridSpec(
            num_scalar_prefetch=1,
            grid=(2, HEADS // PACK_HEADS),
            in_specs=[block, block],
            out_specs=pl.BlockSpec((1, PACK_HEADS, 32, LANES), lambda x, h, place: (x, h, 0, 0)),
        ),
        out_shape=jax.ShapeDtypeStruct((2, HEADS, 32, LANES), jnp.int32),
        name="pack",
    )(place, mine, theirs)


def route_kernel(src_block, group_map, q_slot, words, out, whole_q, where_q):
    r = pl.program_id(0)
    for j in range(GROUP):
        where_q[q_slot[r * GROUP + j]] = j
    lane = lanes_of((8, LANES))
    left = lane < 64
    blocks = [[None] * 10 for _ in range(LAYERS)]
    for pair in range(2):
        even, odd = 2 * pair, 2 * pair + 1
        tiles = {}
        rest = [None] * LAYERS
        for x in range(2):
            third = {}
            for m in (even, odd):
                last = words[x, m, 24:32, :]
                high = high_of(last)
                scales = scale_of(high)
                first = 64 if m == even else 0
                scale = [scales[:, first + l : first + l + 1] for l in range(LAYERS)]
                low = low_of(last).astype(jnp.float32)
                high = high.astype(jnp.float32)
                third[m] = (low * scale[0], low * scale[1], high * scale[2])
                for l in range(LAYERS):
                    word = words[x, m, 8 * l : 8 * l + 8, :]
                    a = low_of(word).astype(jnp.float32) * scale[l]
                    b = high_of(word).astype(jnp.float32) * scale[l]
                    if x == 0:
                        tiles[m, l] = (a, b)
                    else:
                        tiles[m, l] = (tiles[m, l][0] + a, tiles[m, l][1] + b)
            part = [
                jnp.where(left, third[even][0], third[odd][0]),
                jnp.where(left, third[odd][1], third[even][1]),
                jnp.where(left, third[even][2], third[odd][2]),
            ]
            rest = part if x == 0 else [p + q for p, q in zip(rest, part)]
        rest[1] = pltpu.roll(rest[1], 64, 1)
        for l in range(LAYERS):
            blocks[l][5 * pair : 5 * pair + 5] = [
                tiles[even, l][0],
                tiles[even, l][1],
                rest[l],
                tiles[odd, l][0],
                tiles[odd, l][1],
            ]
    codes = []
    for l in range(LAYERS):
        code = codes_of(row_max(*blocks[l]))
        inverse = inverse_scale_of(code)
        codes.append(code)
        for j in range(GROUP):
            whole_q[j, l] = whole(blocks[l][j], inverse)
        key_value = packed(whole(blocks[l][8], inverse), whole(blocks[l][9], inverse))
        for s in range(GROUP_DEVS):
            out[s, 24 + 8 * l : 32 + 8 * l, :] = key_value
    code = jnp.where(lane == 0, codes[0], jnp.where(lane == 1, codes[1], codes[2]))
    for s in range(GROUP_DEVS):
        out[s, 48:56, :] = code
        first, second = where_q[2 * s], where_q[2 * s + 1]
        for l in range(LAYERS):
            out[s, 8 * l : 8 * l + 8, :] = packed(whole_q[first, l], whole_q[second, l])


def route(src_block, group_map, q_slot, words):
    return pl.pallas_call(
        route_kernel,
        grid_spec=pltpu.PrefetchScalarGridSpec(
            num_scalar_prefetch=3,
            grid=(KV_HEADS,),
            in_specs=[
                pl.BlockSpec((2, GROUP_DEVS, 32, LANES), lambda r, src, grp, slot: (0, src[r], 0, 0))
            ],
            out_specs=pl.BlockSpec((GROUP_DEVS, 56, LANES), lambda r, src, grp, slot: (grp[r], 0, 0)),
            scratch_shapes=[
                pltpu.VMEM((GROUP, LAYERS, 8, LANES), jnp.int32),
                pltpu.SMEM((GROUP,), jnp.int32),
            ],
        ),
        out_shape=jax.ShapeDtypeStruct((HEADS, 56, LANES), jnp.int32),
        name="route",
    )(src_block, group_map, q_slot, words)


OPEN_HEADS = 8


def open_kernel(words, out):
    for i in range(OPEN_HEADS):
        scales = scale_of(words[i, 48:56, :])
        rows = slice(8 * i, 8 * i + 8)
        for l in range(LAYERS):
            scale = scales[:, l : l + 1]
            for half in range(2):
                first = 24 * half + 8 * l
                word = words[i, first : first + 8, :]
                cols = 2 * LANES * half
                out[l, rows, cols : cols + LANES] = low_of(word).astype(jnp.float32) * scale
                out[l, rows, cols + LANES : cols + 2 * LANES] = (
                    high_of(word).astype(jnp.float32) * scale
                )


def opened(words):
    return pl.pallas_call(
        open_kernel,
        grid=(HEADS // OPEN_HEADS,),
        in_specs=[pl.BlockSpec((OPEN_HEADS, 56, LANES), lambda h: (h, 0, 0))],
        out_specs=pl.BlockSpec((LAYERS, 8 * OPEN_HEADS, 4 * LANES), lambda h: (0, h, 0)),
        out_shape=jax.ShapeDtypeStruct((LAYERS, SLICE, 4 * LANES), jnp.float32),
        name="opened",
    )(words)


def on_device(hidden, joined_weight, src_block, group_map, q_slot):
    place = jnp.stack([lax.axis_index("core"), lax.axis_index("head") & 1]).astype(jnp.int32)
    weight = jnp.swapaxes(joined_weight, 1, 2)
    away = product(place, hidden, weight, 1)
    theirs = lax.ppermute(away, "core", [(0, 1), (1, 0)])
    mine = product(place, hidden, weight, 0)
    words = pack(place, mine, theirs).reshape(2 * HEADS, 32, LANES)
    words = lax.all_to_all(words, ("near", "head"), 0, 0, tiled=True)
    words = route(src_block, group_map, q_slot, words.reshape(2, HEADS, 32, LANES))
    words = lax.all_to_all(words, "head", 0, 0, tiled=True)
    return opened(words)


def solution(mesh):
    split = Mesh(mesh.devices.reshape(HEADS, 2, 2), ("head", "near", "core"))
    kdim = ("near", "core")
    return jax.shard_map(
        on_device,
        mesh=split,
        in_specs=(P(None, None, kdim), P(None, kdim, "head"), P(), P(), P()),
        out_specs=P(None, kdim, "head"),
        check_vma=False,
    )
```

time: 134 us -> 93.7 us (0.70)
  waiting for transfers between devices: 62.9 us -> 0.01 us
  Pallas kernels: 0 us -> 37.7 us
  blocking collectives: 27.2 us -> 53.1 us
  starting transfers between devices: 15.8 us -> 0.01 us
  matrix products: 13.3 us -> 0 us
  local copies, waits for them, and re-layouts: 11.7 us -> 1.4 us
  other arithmetic: 3.04 us -> 0.65 us
    all_to_all x2 -> x0, waiting for transfers between devices: 62.9 us -> none  [the longest x1 45 us: sent_and_summed(): blocks = lax.all_to_all(cut_along(x, dim, size), axis, 0, 0, tiled=True)]
    pallas_call x0 -> x5, Pallas kernels: none -> 37.7 us  [the longest x2 20 us: product(): pl.pallas_call(product_kernel, grid_spec=pltpu.PrefetchScalarGridSpec(num...]
    all_to_all x1 -> x2, blocking collectives: 27.2 us -> 53.1 us  [the longest x1 31.6 us: on_device(): words = lax.all_to_all(words, ('near', 'head'), 0, 0, tiled=True)]
    all_to_all x2 -> x0, starting transfers between devices: 15.8 us -> none  [the longest x1 10.9 us: on_device(): lax.all_to_all(piece, 'head', split_axis=0, concat_axis=1, tiled=True)]
    dot_general x2 -> x0, matrix products: 13.3 us -> none  [the longest x1 11.9 us: on_device(): jnp.einsum('lrd,ldc->lrc', hidden, joined_weight, preferred_element_type=...]
    reshape x2 -> x0, local copies, waits for them, and re-layouts: 4.99 us -> none  [the longest x1 4.39 us: cut_along(): return jnp.moveaxis(x.reshape(*before, size, -1, *after), dim, 0)]
    reduce_sum x4 -> x0, other arithmetic: 2.73 us -> none  [the longest x1 2.53 us: sent_and_summed(): return jnp.sum(blocks, axis=0)]
    gather x3 -> x0, local copies, waits for them, and re-layouts: 2.01 us -> none  [column_table(): member_slot = q_slot[members]]
  transfers between devices with their start and end apart: 2 -> 1, of which waited for: 2 -> 0; matrix products, arithmetic and copies ran while one was open for 2% -> 0% of each run, Pallas kernels for 0% -> 11%
where the time goes in v1:
time: 93.7 us; the launch traced here: 92.9 us
  blocking collectives  53.1 us (57%)
  Pallas kernels  37.7 us (40%)
  local copies, waits for them, and re-layouts  1.4 us (1%)
    all_to_all x1, blocking collectives, on_device(): words = lax.all_to_all(words, ('near', 'head'), 0, 0, tiled=True)  31.6 us
    all_to_all x1, blocking collectives, on_device(): words = lax.all_to_all(words, 'head', 0, 0, tiled=True)  21.5 us
    pallas_call x2, Pallas kernels, product(): pl.pallas_call(product_kernel, grid_spec=pltpu.PrefetchScalarGridSpec(num...  20 us
    pallas_call x1, Pallas kernels, pack(): pl.pallas_call(pack_kernel, grid_spec=pltpu.PrefetchScalarGridSpec(num_sc...  7.29 us
    pallas_call x1, Pallas kernels, route(): pl.pallas_call(route_kernel, grid_spec=pltpu.PrefetchScalarGridSpec(num_s...  6.83 us
    pallas_call x1, Pallas kernels, opened(): pl.pallas_call(open_kernel, grid=(HEADS // OPEN_HEADS,), in_specs=[pl.Blo...  3.62 us
  transfers between devices with their start and end apart: 1, of which 0 were waited for; matrix products, arithmetic and copies ran while one was open for 0% of the time, Pallas kernels for 11%

profile of v1, /device:TPU:0, one launch (start us, length us, event | category | flops | bytes accessed | tf_op | source)
XLA Modules:
  0.0 92.9 jit_solution(12921231411262610745)
XLA Ops:
  0.0 0.6 pad_add_fusion.place
  0.6 10.0 %product.3 = f32[3,2,256,384]{3,2,1,0:T(8,128)} custom-call(s32[2]{0:T(128)} %pad_add_fusion.place, bf16[3,1024,2048]{2,1,0:T(8,128)(2,1)} %hidden.3, bf16[3,320,2048]{2,1,0:T(8,128)(2,1)} %bitcast.5), custom_call_target="tpu_custom_call" | custom-call | flops 2013265920 | bytes 12000000 | tf_op jit(solution)/shard_map/product/pallas_call | solution.py:84
  10.6 0.0 collective-permute-start
  10.6 10.0 %product.2.mine = f32[3,2,256,384]{3,2,1,0:T(8,128)} custom-call(s32[2]{0:T(128)} %pad_add_fusion.place, bf16[3,1024,2048]{2,1,0:T(8,128)(2,1)} %hidden.3, bf16[3,320,2048]{2,1,0:T(8,128)(2,1)} %bitcast.6), custom_call_target="tpu_custom_call" | custom-call | flops 2013265920 | bytes 12000000 | tf_op jit(solution)/shard_map/product/pallas_call | solution.py:84
  20.6 0.0 collective-permute-done.theirs
  20.6 0.0 copy-start
  20.6 1.4 %copy-done = f32[3,2,256,384]{3,2,1,0:T(8,128)} copy-done((f32[3,2,256,384]{3,2,1,0:T(8,128)}, f32[3,2,256,384]{3,2,1,0:T(8,128)S(1)}, u32[]{:S(2)}) %copy-start) | copy-done | bytes 2359320
  22.0 7.3 %pack.1 = s32[2,32,32,128]{3,2,1,0:T(8,128)} custom-call(s32[2]{0:T(128)} %pad_add_fusion.place, f32[3,2,256,384]{3,2,1,0:T(8,128)} %product.2.mine, f32[3,2,256,384]{3,2,1,0:T(8,128)} %copy-done), custom_call_target="tpu_custom_call" | custom-call | tf_op jit(solution)/shard_map/pack/pallas_call | solution.py:133
  29.3 31.6 %all_to_all.10 = s32[64,32,128]{2,1,0:T(8,128)} all-to-all(s32[64,32,128]{2,1,0:T(8,128)} %bitcast.8), channel_id=1, replica_groups=mesh['head'=32,'near'=2,'core'=2] {'near','head'}, dimensions={0} | all-to-all | bytes 2097152 | tf_op jit(solution)/shard_map/all_to_all | solution.py:266
  60.9 6.8 %route.1 = s32[32,56,128]{2,1,0:T(8,128)} custom-call(s32[8]{0:T(128)} %src_block.1, s32[8]{0:T(128)} %group_map.1, s32[64]{0:T(128)} %q_slot.1, s32[2,32,32,128]{3,2,1,0:T(8,128)} %bitcast.7), custom_call_target="tpu_custom_call" | custom-call | tf_op jit(solution)/shard_map/route/pallas_call | solution.py:210
  67.7 21.5 %all_to_all.11.words = s32[32,56,128]{2,1,0:T(8,128)} all-to-all(s32[32,56,128]{2,1,0:T(8,128)} %route.1), channel_id=1, replica_groups=mesh['head'=32,'near'=2,'core'=2] {'head'}, dimensions={0} | all-to-all | bytes 1835008 | tf_op jit(solution)/shard_map/all_to_all | solution.py:268
  89.3 3.6 %opened.1 = f32[3,256,512]{2,1,0:T(8,128)} custom-call(s32[32,56,128]{2,1,0:T(8,128)} %all_to_all.11.words), custom_call_target="tpu_custom_call" | custom-call | tf_op jit(solution)/shard_map/opened/pallas_call | solution.py:249
Async XLA Ops:
  10.6 10.0 %collective-permute-start = (f32[3,2,256,384]{3,2,1,0:T(8,128)}, f32[3,2,256,384]{3,2,1,0:T(8,128)S(1)}, u32[]{:S(2)}, u32[]{:S(2)}) collective-permute-start(f32[3,2,256,384]{3,2,1,0:T(8,128)} %product.3), channel_id=1, source_target_pairs={{0,1},{1,0},{2,3},{3,2},{4,5},{5,4},{6,7},{7,6},{8,9},{9,8},{10,11... | collective-permute-start | bytes 7077896 | tf_op jit(solution)/shard_map/ppermute | solution.py:263
  20.6 1.4 %copy-start = (f32[3,2,256,384]{3,2,1,0:T(8,128)}, f32[3,2,256,384]{3,2,1,0:T(8,128)S(1)}, u32[]{:S(2)}) copy-start(f32[3,2,256,384]{3,2,1,0:T(8,128)S(1)} %collective-permute-done.theirs) | copy-start | bytes 7077892

commit v2 on v1

v2 whole, which is shorter than its diff:
```python
import jax
import jax.numpy as jnp
from jax import lax
from jax.experimental import pallas as pl
from jax.experimental.pallas import tpu as pltpu
from jax.sharding import Mesh, PartitionSpec as P

LAYERS = 3
ROWS = 1024
SLICE = 256
LANES = 128
WIDTH = 320
PADDED = 384
HEADS = 32
GROUP_DEVS = 4
KV_HEADS = 8
GROUP = 8
CODES = 256.0
TOP = 32700.0


def codes_of(amax):
    return jnp.ceil(CODES * jnp.log2(jnp.maximum(amax, 1e-30) * (1.0 / TOP))).astype(jnp.int32)


def scale_of(code):
    return jnp.exp2(code.astype(jnp.float32) * (1.0 / CODES))


def inverse_scale_of(code):
    return jnp.exp2(code.astype(jnp.float32) * (-1.0 / CODES))


def whole(x, inverse):
    return jnp.round(x * inverse).astype(jnp.int32)


def packed(low, high):
    return (low & 0xFFFF) | (high << 16)


def low_of(words):
    return (words << 16) >> 16


def high_of(words):
    return words >> 16


def row_max(*tiles):
    top = jnp.abs(tiles[0])
    for tile in tiles[1:]:
        top = jnp.maximum(top, jnp.abs(tile))
    return jnp.max(top, axis=1, keepdims=True)


def lanes_of(shape):
    return lax.broadcasted_iota(jnp.int32, shape, 1)


VMEM = pl.BlockSpec(memory_space=pltpu.VMEM)
SMEM = pl.BlockSpec(memory_space=pltpu.SMEM)
HBM = pl.BlockSpec(memory_space=pltpu.HBM)


def limit(mib, **others):
    return pltpu.CompilerParams(vmem_limit_bytes=mib * 1024 * 1024, **others)


def placed(value, odd, out):
    @pl.when(odd == 0)
    def _():
        out[:, :WIDTH] = value
        out[:, WIDTH:] = jnp.zeros((2 * SLICE, PADDED - WIDTH), jnp.float32)

    @pl.when(odd == 1)
    def _():
        out[:, :256] = value[:, 64:]
        out[:, 256:320] = jnp.zeros((2 * SLICE, 64), jnp.float32)
        out[:, 320:] = value[:, :64]


def product_of(rows, weight):
    return lax.dot_general(
        rows, weight, (((1,), (1,)), ((), ())), preferred_element_type=jnp.float32
    )


def away_kernel(place, hidden, weight, out, my_rows, weight_rows, away_rows, arrived):
    core = place[0]

    def rows_copy(l, x, other):
        first = pl.multiple_of((2 * x + (1 - core if other else core)) * SLICE, SLICE)
        target = away_rows if other else my_rows
        return pltpu.make_async_copy(
            hidden.at[l, pl.ds(first, SLICE), :],
            target.at[l, pl.ds(SLICE * x, SLICE), :],
            arrived.at[l, 2 * int(other) + x],
        )

    def weight_copy(l):
        return pltpu.make_async_copy(weight.at[l], weight_rows.at[l], arrived.at[l, 4])

    for l in range(LAYERS):
        weight_copy(l).start()
        for x in range(2):
            rows_copy(l, x, True).start()
    for l in range(LAYERS):
        for x in range(2):
            rows_copy(l, x, False).start()

    @pl.loop(0, LAYERS)
    def _(l):
        weight_copy(l).wait()
        for x in range(2):
            rows_copy(l, x, True).wait()
        placed(product_of(away_rows[l], weight_rows[l]), place[1], out.at[l])

    for l in range(LAYERS):
        for x in range(2):
            rows_copy(l, x, False).wait()


def away_product(place, hidden, weight):
    return pl.pallas_call(
        away_kernel,
        in_specs=[SMEM, HBM, HBM],
        out_specs=[VMEM, VMEM, VMEM],
        scratch_shapes=[
            pltpu.VMEM((LAYERS, 2 * SLICE, 2048), jnp.bfloat16),
            pltpu.SemaphoreType.DMA((LAYERS, 5)),
        ],
        out_shape=[
            pltpu.VMEM((LAYERS, 2 * SLICE, PADDED), jnp.float32),
            pltpu.VMEM((LAYERS, 2 * SLICE, 2048), jnp.bfloat16),
            pltpu.VMEM((LAYERS, WIDTH, 2048), jnp.bfloat16),
        ],
        cost_estimate=pl.CostEstimate(
            flops=LAYERS * 512 * 2048 * WIDTH * 2, bytes_accessed=20_000_000, transcendentals=0
        ),
        compiler_params=limit(44),
        name="away_product",
    )(place, hidden, weight)


def my_kernel(place, rows, weight, out):
    @pl.loop(0, LAYERS)
    def _(l):
        placed(product_of(rows[l], weight[l]), place[1], out.at[l])


def my_product(place, rows, weight):
    return pl.pallas_call(
        my_kernel,
        in_specs=[SMEM, VMEM, VMEM],
        out_specs=VMEM,
        out_shape=jax.ShapeDtypeStruct((LAYERS, 2 * SLICE, PADDED), jnp.float32),
        cost_estimate=pl.CostEstimate(
            flops=LAYERS * 512 * 2048 * WIDTH * 2, bytes_accessed=12_000_000, transcendentals=0
        ),
        compiler_params=limit(24),
        name="my_product",
    )(place, rows, weight)


PACK_HEADS = 8


def pack_kernel(place, mine, theirs, out):
    odd = place[1]
    lane = lanes_of((8, LANES))
    spare = (lane >= 64) != (odd == 1)
    slot = lane & 63
    step = pl.program_id(0)
    for i in range(PACK_HEADS):
        rows = pl.ds(pl.multiple_of(8 * (step * PACK_HEADS + i), 8), 8)
        block = step * PACK_HEADS + i
        rest, codes = [], []
        for l in range(LAYERS):
            tiles = []
            for t in range(3):
                cols = slice(LANES * t, LANES * t + LANES)
                tiles.append(mine[l, rows, cols] + theirs[l, rows, cols])
            code = codes_of(row_max(*tiles))
            inverse = inverse_scale_of(code)
            a, b, c = [whole(tile, inverse) for tile in tiles]
            out[block, 8 * l : 8 * l + 8, :] = packed(a, b)
            rest.append(c)
            codes.append(code)
        code = jnp.where(slot == 0, codes[0], jnp.where(slot == 1, codes[1], codes[2]))
        low = rest[0] + pltpu.roll(rest[1], 64, 1)
        high = jnp.where(spare, code, rest[2])
        out[block, 24:32, :] = packed(low, high)


def pack(place, mine, theirs):
    return pl.pallas_call(
        pack_kernel,
        grid=(2 * HEADS // PACK_HEADS,),
        in_specs=[SMEM, VMEM, VMEM],
        out_specs=VMEM,
        out_shape=jax.ShapeDtypeStruct((2 * HEADS, 32, LANES), jnp.int32),
        compiler_params=limit(16),
        name="pack",
    )(place, mine, theirs)


def route_kernel(src_block, group_map, q_slot, words, out, whole_q, where_q):
    r = pl.program_id(0)
    source = src_block[r] * GROUP_DEVS
    target = group_map[r] * GROUP_DEVS
    for j in range(GROUP):
        where_q[q_slot[r * GROUP + j]] = j
    lane = lanes_of((8, LANES))
    left = lane < 64
    blocks = [[None] * 10 for _ in range(LAYERS)]
    for pair in range(2):
        even, odd = 2 * pair, 2 * pair + 1
        tiles = {}
        rest = [None] * LAYERS
        for x in range(2):
            third = {}
            for m in (even, odd):
                last = words[x * HEADS + source + m, 24:32, :]
                high = high_of(last)
                scales = scale_of(high)
                first = 64 if m == even else 0
                scale = [scales[:, first + l : first + l + 1] for l in range(LAYERS)]
                low = low_of(last).astype(jnp.float32)
                high = high.astype(jnp.float32)
                third[m] = (low * scale[0], low * scale[1], high * scale[2])
                for l in range(LAYERS):
                    word = words[x * HEADS + source + m, 8 * l : 8 * l + 8, :]
                    a = low_of(word).astype(jnp.float32) * scale[l]
                    b = high_of(word).astype(jnp.float32) * scale[l]
                    if x == 0:
                        tiles[m, l] = (a, b)
                    else:
                        tiles[m, l] = (tiles[m, l][0] + a, tiles[m, l][1] + b)
            part = [
                jnp.where(left, third[even][0], third[odd][0]),
                jnp.where(left, third[odd][1], third[even][1]),
                jnp.where(left, third[even][2], third[odd][2]),
            ]
            rest = part if x == 0 else [p + q for p, q in zip(rest, part)]
        rest[1] = pltpu.roll(rest[1], 64, 1)
        for l in range(LAYERS):
            blocks[l][5 * pair : 5 * pair + 5] = [
                tiles[even, l][0],
                tiles[even, l][1],
                rest[l],
                tiles[odd, l][0],
                tiles[odd, l][1],
            ]
    codes = []
    for l in range(LAYERS):
        code = codes_of(row_max(*blocks[l]))
        inverse = inverse_scale_of(code)
        codes.append(code)
        for j in range(GROUP):
            whole_q[j, l] = whole(blocks[l][j], inverse)
        key_value = packed(whole(blocks[l][8], inverse), whole(blocks[l][9], inverse))
        for s in range(GROUP_DEVS):
            out[target + s, 24 + 8 * l : 32 + 8 * l, :] = key_value
    code = jnp.where(lane == 0, codes[0], jnp.where(lane == 1, codes[1], codes[2]))
    for s in range(GROUP_DEVS):
        out[target + s, 48:56, :] = code
        first, second = where_q[2 * s], where_q[2 * s + 1]
        for l in range(LAYERS):
            out[target + s, 8 * l : 8 * l + 8, :] = packed(whole_q[first, l], whole_q[second, l])


def route(src_block, group_map, q_slot, words):
    return pl.pallas_call(
        route_kernel,
        grid=(KV_HEADS,),
        in_specs=[SMEM, SMEM, SMEM, VMEM],
        out_specs=VMEM,
        scratch_shapes=[
            pltpu.VMEM((GROUP, LAYERS, 8, LANES), jnp.int32),
            pltpu.SMEM((GROUP,), jnp.int32),
        ],
        out_shape=jax.ShapeDtypeStruct((HEADS, 56, LANES), jnp.int32),
        compiler_params=limit(16),
        name="route",
    )(src_block, group_map, q_slot, words)


OPEN_HEADS = 8


def open_kernel(words, out):
    for i in range(OPEN_HEADS):
        block = pl.program_id(0) * OPEN_HEADS + i
        scales = scale_of(words[block, 48:56, :])
        rows = slice(8 * i, 8 * i + 8)
        for l in range(LAYERS):
            scale = scales[:, l : l + 1]
            for half in range(2):
                first = 24 * half + 8 * l
                word = words[block, first : first + 8, :]
                cols = 2 * LANES * half
                out[l, rows, cols : cols + LANES] = low_of(word).astype(jnp.float32) * scale
                out[l, rows, cols + LANES : cols + 2 * LANES] = (
                    high_of(word).astype(jnp.float32) * scale
                )


def opened(words):
    return pl.pallas_call(
        open_kernel,
        grid=(HEADS // OPEN_HEADS,),
        in_specs=[VMEM],
        out_specs=pl.BlockSpec((LAYERS, 8 * OPEN_HEADS, 4 * LANES), lambda h: (0, h, 0)),
        out_shape=jax.ShapeDtypeStruct((LAYERS, SLICE, 4 * LANES), jnp.float32),
        compiler_params=limit(16),
        name="opened",
    )(words)


def on_device(hidden, joined_weight, src_block, group_map, q_slot):
    place = jnp.stack([lax.axis_index("core"), lax.axis_index("head") & 1]).astype(jnp.int32)
    hidden = pltpu.with_memory_space_constraint(hidden, pltpu.HBM)
    weight = pltpu.with_memory_space_constraint(jnp.swapaxes(joined_weight, 1, 2), pltpu.HBM)
    away, rows, weight = away_product(place, hidden, weight)
    theirs = lax.ppermute(away, "core", [(0, 1), (1, 0)])
    mine = my_product(place, rows, weight)
    words = pack(place, mine, theirs)
    words = lax.all_to_all(words, ("near", "head"), 0, 0, tiled=True)
    words = route(src_block, group_map, q_slot, words)
    words = lax.all_to_all(words, "head", 0, 0, tiled=True)
    return opened(words)


def solution(mesh):
    split = Mesh(mesh.devices.reshape(HEADS, 2, 2), ("head", "near", "core"))
    kdim = ("near", "core")
    return jax.shard_map(
        on_device,
        mesh=split,
        in_specs=(P(None, None, kdim), P(None, kdim, "head"), P(), P(), P()),
        out_specs=P(None, kdim, "head"),
        check_vma=False,
    )
```

time: 93.7 us -> 72.3 us (0.77)
  Pallas kernels: 37.7 us -> 18.4 us
  local copies, waits for them, and re-layouts: 1.4 us -> 0.02 us
    pallas_call x5, Pallas kernels: 37.7 us -> 18.4 us  [the longest x1 6.83 us: away_product(): pl.pallas_call(away_kernel, in_specs=[SMEM, HBM, HBM], out_specs=[VMEM, V...]
    unnamed x2 -> x8, local copies, waits for them, and re-layouts: 1.4 us -> 0.02 us
  transfers between devices with their start and end apart: 1 -> 1, of which waited for: 0 -> 0; matrix products, arithmetic and copies ran while one was open for 0% -> 0% of each run, Pallas kernels for 11% -> 6%
where the time goes in v2:
time: 72.3 us; the launch traced here: 72.2 us
  blocking collectives  52.9 us (73%)
  Pallas kernels  18.4 us (25%)
    all_to_all x1, blocking collectives, on_device(): words = lax.all_to_all(words, ('near', 'head'), 0, 0, tiled=True)  32 us
    all_to_all x1, blocking collectives, on_device(): words = lax.all_to_all(words, 'head', 0, 0, tiled=True)  21 us
    pallas_call x1, Pallas kernels, away_product(): pl.pallas_call(away_kernel, in_specs=[SMEM, HBM, HBM], out_specs=[VMEM, V...  6.83 us
    pallas_call x1, Pallas kernels, my_product(): pl.pallas_call(my_kernel, in_specs=[SMEM, VMEM, VMEM], out_specs=VMEM, ou...  4.51 us
    pallas_call x1, Pallas kernels, route(): pl.pallas_call(route_kernel, grid=(KV_HEADS,), in_specs=[SMEM, SMEM, SMEM...  2.86 us
    pallas_call x1, Pallas kernels, pack(): pl.pallas_call(pack_kernel, grid=(2 * HEADS // PACK_HEADS,), in_specs=[SM...  2.32 us
    pallas_call x1, Pallas kernels, opened(): pl.pallas_call(open_kernel, grid=(HEADS // OPEN_HEADS,), in_specs=[VMEM],...  1.85 us
  transfers between devices with their start and end apart: 1, of which 0 were waited for; matrix products, arithmetic and copies ran while one was open for 0% of the time, Pallas kernels for 6%

profile of v2, /device:TPU:0, one launch (start us, length us, event | category | flops | bytes accessed | tf_op | source)
XLA Modules:
  0.0 72.2 jit_solution(11644927190208930427)
XLA Ops:
  0.0 0.7 pad_add_fusion.place
  0.7 0.0 copy-start
  0.7 6.8 %away_product.1 = (f32[3,512,384]{2,1,0:T(8,128)S(1)}, bf16[3,512,2048]{2,1,0:T(8,128)(2,1)S(1)}, bf16[3,320,2048]{2,1,0:T(8,128)(2,1)S(1)}) custom-call(s32[2]{0:T(128)} %pad_add_fusion.place, bf16[3,1024,2048]{2,1,0:T(8,128)(2,1)} %hidden.1, bf16[3,320,2048]{2,1,0:T(8,128)(2,1)} %bitcast.3), custom_call_target="tpu_custom_call" | custom-call | flops 2013265920 | bytes 20000000 | tf_op jit(solution)/shard_map/away_product/pallas_call | solution.py:125
  7.5 0.1 collective-permute-start
  7.6 0.0 copy-done
  7.6 4.5 %my_product.1.mine = f32[3,512,384]{2,1,0:T(8,128)S(1)} custom-call(s32[2]{0:T(128)S(1)} %copy-done, bf16[3,512,2048]{2,1,0:T(8,128)(2,1)S(1)} %get-tuple-element.8.rows, bf16[3,320,2048]{2,1,0:T(8,128)(2,1)S(1)} %get-tuple-element.9.weight), custom_call_target="tpu_custom_call" | custom-call | flops 2013265920 | bytes 12000000 | tf_op jit(solution)/shard_map/my_product/pallas_call | solution.py:153
  12.1 0.0 copy-start.1
  12.1 0.0 copy-start.2
  12.2 0.0 copy-start.3
  12.2 0.0 collective-permute-done.theirs
  12.2 2.3 %pack.1 = s32[64,32,128]{2,1,0:T(8,128)S(1)} custom-call(s32[2]{0:T(128)S(1)} %copy-done, f32[3,512,384]{2,1,0:T(8,128)S(1)} %my_product.1.mine, f32[3,512,384]{2,1,0:T(8,128)S(1)} %collective-permute-done.theirs), custom_call_target="tpu_custom_call" | custom-call | tf_op jit(solution)/shard_map/pack/pallas_call | solution.py:197
  14.5 32.0 %all_to_all.10.words = s32[64,32,128]{2,1,0:T(8,128)S(1)} all-to-all(s32[64,32,128]{2,1,0:T(8,128)S(1)} %pack.1), channel_id=1, replica_groups=mesh['head'=32,'near'=2,'core'=2] {'near','head'}, dimensions={0} | all-to-all | bytes 2097152 | tf_op jit(solution)/shard_map/all_to_all | solution.py:329
  46.4 0.0 copy-done.1
  46.5 0.0 copy-done.2
  46.5 0.0 copy-done.3
  46.5 2.9 %route.1 = s32[32,56,128]{2,1,0:T(8,128)S(1)} custom-call(s32[8]{0:T(128)S(1)} %copy-done.1, s32[8]{0:T(128)S(1)} %copy-done.2, s32[64]{0:T(128)S(1)} %copy-done.3, s32[64,32,128]{2,1,0:T(8,128)S(1)} %all_to_all.10.words), custom_call_target="tpu_custom_call" | custom-call | tf_op jit(solution)/shard_map/route/pallas_call | solution.py:274
  49.3 21.0 %all_to_all.11.words = s32[32,56,128]{2,1,0:T(8,128)S(1)} all-to-all(s32[32,56,128]{2,1,0:T(8,128)S(1)} %route.1), channel_id=1, replica_groups=mesh['head'=32,'near'=2,'core'=2] {'head'}, dimensions={0} | all-to-all | bytes 1835008 | tf_op jit(solution)/shard_map/all_to_all | solution.py:331
  70.3 1.8 %opened.1 = f32[3,256,512]{2,1,0:T(8,128)} custom-call(s32[32,56,128]{2,1,0:T(8,128)S(1)} %all_to_all.11.words), custom_call_target="tpu_custom_call" | custom-call | tf_op jit(solution)/shard_map/opened/pallas_call | solution.py:310
Async XLA Ops:
  0.7 6.9 %copy-start = (s32[2]{0:T(128)S(1)}, s32[2]{0:T(128)}, u32[]{:S(2)}) copy-start(s32[2]{0:T(128)} %pad_add_fusion.place) | copy-start | bytes 28
  7.5 4.7 %collective-permute-start = (f32[3,512,384]{2,1,0:T(8,128)S(1)}, f32[3,512,384]{2,1,0:T(8,128)S(1)}, u32[]{:S(2)}, u32[]{:S(2)}) collective-permute-start(f32[3,512,384]{2,1,0:T(8,128)S(1)} %get-tuple-element.10), channel_id=1, source_target_pairs={{0,1},{1,0},{2,3},{3,2},{4,5},{5,4},{6,7},{7,6},{8,9},{9,8},{10,11... | collective-permute-start | bytes 7077896 | tf_op jit(solution)/shard_map/ppermute | solution.py:326
  12.1 34.3 %copy-start.1 = (s32[8]{0:T(128)S(1)}, s32[8]{0:T(128)}, u32[]{:S(2)}) copy-start(s32[8]{0:T(128)} %src_block.1) | copy-start | bytes 100
  12.1 34.3 %copy-start.2 = (s32[8]{0:T(128)S(1)}, s32[8]{0:T(128)}, u32[]{:S(2)}) copy-start(s32[8]{0:T(128)} %group_map.1) | copy-start | bytes 100
  12.2 34.3 %copy-start.3 = (s32[64]{0:T(128)S(1)}, s32[64]{0:T(128)}, u32[]{:S(2)}) copy-start(s32[64]{0:T(128)} %q_slot.1) | copy-start | bytes 772

commit v3 on v2

v3 whole, which is shorter than its diff:
```python
import jax
import jax.numpy as jnp
from jax import lax
from jax.experimental import pallas as pl
from jax.experimental.pallas import tpu as pltpu
from jax.sharding import Mesh, PartitionSpec as P

LAYERS = 3
SLICE = 256
MINE = 2 * SLICE
DEPTH = 2048
LANES = 128
WIDTH = 320
PADDED = 384
HEADS = 32
GROUP_DEVS = 4
KV_HEADS = 8
GROUP = 8
CODES = 256.0
TOP = 32700.0

VMEM = pl.BlockSpec(memory_space=pltpu.VMEM)
SMEM = pl.BlockSpec(memory_space=pltpu.SMEM)
HBM = pl.BlockSpec(memory_space=pltpu.HBM)


def limit(mib):
    return pltpu.CompilerParams(vmem_limit_bytes=mib * 1024 * 1024)


def codes_of(amax):
    return jnp.ceil(CODES * jnp.log2(jnp.maximum(amax, 1e-30) * (1.0 / TOP))).astype(jnp.int32)


def scale_of(code):
    return jnp.exp2(code.astype(jnp.float32) * (1.0 / CODES))


def inverse_scale_of(code):
    return jnp.exp2(code.astype(jnp.float32) * (-1.0 / CODES))


def whole(x):
    return jnp.round(x).astype(jnp.int32)


def packed(low, high):
    return (low & 0xFFFF) | (high << 16)


def low_of(words):
    return (words << 16) >> 16


def high_of(words):
    return words >> 16


def lanes():
    return lax.broadcasted_iota(jnp.int32, (8, LANES), 1)


def product_of(rows, weight):
    return lax.dot_general(
        rows, weight, (((1,), (1,)), ((), ())), preferred_element_type=jnp.float32
    )


def away_kernel(hidden, weight, out, my_rows, weight_rows, away_rows, arrived):
    core = lax.axis_index("core")
    odd = lax.axis_index("head") & 1

    def rows_copy(l, x, other):
        first = pl.multiple_of((2 * x + (1 - core if other else core)) * SLICE, SLICE)
        target = away_rows if other else my_rows
        return pltpu.make_async_copy(
            hidden.at[l, pl.ds(first, SLICE), :],
            target.at[l, pl.ds(SLICE * x, SLICE), :],
            arrived.at[l, 2 * int(other) + x],
        )

    def weight_copies(l):
        blocks = pl.multiple_of(64 * odd, 64)
        half = pl.multiple_of(256 * (1 - odd), 64)
        place = pl.multiple_of(256 + 64 * odd, 64)
        return [
            pltpu.make_async_copy(
                weight.at[l, pl.ds(blocks, 256), :],
                weight_rows.at[l, pl.ds(0, 256), :],
                arrived.at[l, 4],
            ),
            pltpu.make_async_copy(
                weight.at[l, pl.ds(half, 64), :],
                weight_rows.at[l, pl.ds(place, 64), :],
                arrived.at[l, 5],
            ),
        ]

    for l in range(LAYERS):
        for copy in weight_copies(l):
            copy.start()
        for x in range(2):
            rows_copy(l, x, True).start()
    for l in range(LAYERS):
        for x in range(2):
            rows_copy(l, x, False).start()
    nothing = pl.multiple_of(320 - 64 * odd, 64)
    for l in range(LAYERS):
        weight_rows[l, pl.ds(nothing, 64), :] = jnp.zeros((64, DEPTH), jnp.bfloat16)

    @pl.loop(0, LAYERS)
    def _(l):
        for copy in weight_copies(l):
            copy.wait()
        for x in range(2):
            rows_copy(l, x, True).wait()
        out[l] = product_of(away_rows[l], weight_rows[l])

    for l in range(LAYERS):
        for x in range(2):
            rows_copy(l, x, False).wait()


def away_product(hidden, weight):
    return pl.pallas_call(
        away_kernel,
        in_specs=[HBM, HBM],
        out_specs=[VMEM, VMEM, VMEM],
        scratch_shapes=[
            pltpu.VMEM((LAYERS, MINE, DEPTH), jnp.bfloat16),
            pltpu.SemaphoreType.DMA((LAYERS, 6)),
        ],
        out_shape=[
            pltpu.VMEM((LAYERS, MINE, PADDED), jnp.float32),
            pltpu.VMEM((LAYERS, MINE, DEPTH), jnp.bfloat16),
            pltpu.VMEM((LAYERS, PADDED, DEPTH), jnp.bfloat16),
        ],
        cost_estimate=pl.CostEstimate(
            flops=LAYERS * MINE * DEPTH * PADDED * 2, bytes_accessed=20_000_000, transcendentals=0
        ),
        compiler_params=limit(44),
        name="away_product",
    )(hidden, weight)


def my_kernel(rows, weight, out):
    @pl.loop(0, LAYERS)
    def _(l):
        out[l] = product_of(rows[l], weight[l])


def my_product(rows, weight):
    return pl.pallas_call(
        my_kernel,
        in_specs=[VMEM, VMEM],
        out_specs=VMEM,
        out_shape=pltpu.VMEM((LAYERS, MINE, PADDED), jnp.float32),
        cost_estimate=pl.CostEstimate(
            flops=LAYERS * MINE * DEPTH * PADDED * 2, bytes_accessed=12_000_000, transcendentals=0
        ),
        compiler_params=limit(24),
        name="my_product",
    )(rows, weight)


PACK_UNROLL = 8


def pack_kernel(mine, theirs, out):
    lane = lanes()
    odd = lax.axis_index("head") & 1
    spare = (lane >= 64) != (odd == 1)
    slot = lane & 63
    for x in range(2):

        def pack_tiles(step, codes):
            for i in range(PACK_UNROLL):
                head = step * PACK_UNROLL + i
                block = x * HEADS + head
                rows = pl.ds(pl.multiple_of(8 * block, 8), 8)
                tiles = [mine[l, rows, :] + theirs[l, rows, :] for l in range(LAYERS)]
                top = jnp.maximum(
                    jnp.maximum(jnp.abs(tiles[0]), jnp.abs(tiles[1])), jnp.abs(tiles[2])
                )
                code = codes_of(jnp.max(top, axis=1, keepdims=True))
                inverse = inverse_scale_of(code)
                rest = []
                for l in range(LAYERS):
                    a, b, c = [
                        whole(tiles[l][:, LANES * t : LANES * t + LANES] * inverse)
                        for t in range(3)
                    ]
                    out[block, 8 * l : 8 * l + 8, :] = packed(a, b)
                    rest.append(c)
                low = rest[0] + pltpu.roll(rest[1], 64, 1)
                out[block, 24:32, :] = packed(low, jnp.where(spare, code, rest[2]))
                codes = jnp.where(slot == head, code, codes)
            return codes

        codes = lax.fori_loop(
            0, HEADS // PACK_UNROLL, pack_tiles, jnp.zeros((8, LANES), jnp.int32)
        )
        codes = codes << 16
        shown = spare & (slot < HEADS)

        @pl.loop(0, HEADS // PACK_UNROLL)
        def _(step):
            for i in range(PACK_UNROLL):
                block = x * HEADS + step * PACK_UNROLL + i
                word = out[block, 24:32, :]
                out[block, 24:32, :] = jnp.where(shown, (word & 0xFFFF) | codes, word)


def pack(mine, theirs):
    return pl.pallas_call(
        pack_kernel,
        in_specs=[VMEM, VMEM],
        out_specs=VMEM,
        out_shape=pltpu.VMEM((2 * HEADS, 32, LANES), jnp.int32),
        compiler_params=limit(16),
        name="pack",
    )(mine, theirs)


def route_kernel(table, words, out, scales, whole_q, where_q):
    reach = []
    for x in range(2):
        tops = []
        for parity in range(2):
            top = None
            for m in range(parity, HEADS, 2):
                code = high_of(words[x * HEADS + m, 24:32, :])
                top = code if top is None else jnp.maximum(top, code)
            tops.append(top)
        reach.append(scale_of(jnp.maximum(tops[0], pltpu.roll(tops[1], 64, 1))))
    reach = reach[0] + reach[1]
    scales[...] = reach
    inverse = 1.0 / reach[:, 96:97]
    left = lanes() < 64

    @pl.loop(0, KV_HEADS)
    def _(r):
        source = table[r] * GROUP_DEVS
        target = table[KV_HEADS + r] * GROUP_DEVS
        for j in range(GROUP):
            where_q[table[2 * KV_HEADS + r * GROUP + j]] = j
        blocks = [[None] * 10 for _ in range(LAYERS)]
        for pair in range(2):
            even, odd = 2 * pair, 2 * pair + 1
            tiles = {}
            rest = None
            for x in range(2):
                third = {}
                for m in (even, odd):
                    device = x * HEADS + source + m
                    last = words[device, 24:32, :]
                    low, high = low_of(last), high_of(last)
                    at = 96 if m == even else 32
                    ratio = scale_of(high[:, at : at + 1]) * inverse
                    third[m] = (low.astype(jnp.float32) * ratio, high.astype(jnp.float32) * ratio)
                    for l in range(LAYERS):
                        word = words[device, 8 * l : 8 * l + 8, :]
                        a = low_of(word).astype(jnp.float32) * ratio
                        b = high_of(word).astype(jnp.float32) * ratio
                        if x == 0:
                            tiles[m, l] = (a, b)
                        else:
                            tiles[m, l] = (tiles[m, l][0] + a, tiles[m, l][1] + b)
                part = [
                    jnp.where(left, third[even][0], third[odd][0]),
                    jnp.where(left, third[odd][0], third[even][0]),
                    jnp.where(left, third[even][1], third[odd][1]),
                ]
                rest = part if x == 0 else [p + q for p, q in zip(rest, part)]
            rest[1] = pltpu.roll(rest[1], 64, 1)
            for l in range(LAYERS):
                blocks[l][5 * pair : 5 * pair + 5] = [
                    tiles[even, l][0],
                    tiles[even, l][1],
                    rest[l],
                    tiles[odd, l][0],
                    tiles[odd, l][1],
                ]
        for l in range(LAYERS):
            for j in range(GROUP):
                whole_q[j, l] = whole(blocks[l][j])
            key_value = packed(whole(blocks[l][8]), whole(blocks[l][9]))
            for s in range(GROUP_DEVS):
                out[target + s, 24 + 8 * l : 32 + 8 * l, :] = key_value
        for s in range(GROUP_DEVS):
            first, second = where_q[2 * s] & 7, where_q[2 * s + 1] & 7
            for l in range(LAYERS):
                out[target + s, 8 * l : 8 * l + 8, :] = packed(whole_q[first, l], whole_q[second, l])


def route(table, words):
    return pl.pallas_call(
        route_kernel,
        in_specs=[SMEM, VMEM],
        out_specs=[VMEM, VMEM],
        scratch_shapes=[
            pltpu.VMEM((GROUP, LAYERS, 8, LANES), jnp.int32),
            pltpu.SMEM((GROUP,), jnp.int32),
        ],
        out_shape=[
            pltpu.VMEM((HEADS, 48, LANES), jnp.int32),
            pltpu.VMEM((8, LANES), jnp.float32),
        ],
        compiler_params=limit(16),
        name="route",
    )(table, words)


OPEN_HEADS = 8


def open_kernel(words, scales, out):
    step = pl.program_id(0)
    scale_columns = pltpu.roll(scales[...], 64 - OPEN_HEADS * step, 1)
    for i in range(OPEN_HEADS):
        block = step * OPEN_HEADS + i
        scale = scale_columns[:, i : i + 1]
        rows = slice(8 * i, 8 * i + 8)
        for l in range(LAYERS):
            for half in range(2):
                first = 24 * half + 8 * l
                word = words[block, first : first + 8, :]
                cols = 2 * LANES * half
                out[l, rows, cols : cols + LANES] = low_of(word).astype(jnp.float32) * scale
                out[l, rows, cols + LANES : cols + 2 * LANES] = (
                    high_of(word).astype(jnp.float32) * scale
                )


def opened(words, scales):
    return pl.pallas_call(
        open_kernel,
        grid=(HEADS // OPEN_HEADS,),
        in_specs=[VMEM, VMEM],
        out_specs=pl.BlockSpec((LAYERS, 8 * OPEN_HEADS, 4 * LANES), lambda h: (0, h, 0)),
        out_shape=jax.ShapeDtypeStruct((LAYERS, SLICE, 4 * LANES), jnp.float32),
        compiler_params=limit(16),
        name="opened",
    )(words, scales)


def on_device(hidden, joined_weight, src_block, group_map, q_slot):
    hidden = pltpu.with_memory_space_constraint(hidden, pltpu.HBM)
    weight = pltpu.with_memory_space_constraint(jnp.swapaxes(joined_weight, 1, 2), pltpu.HBM)
    away, rows, weight = away_product(hidden, weight)
    theirs = lax.ppermute(away, "core", [(0, 1), (1, 0)])
    mine = my_product(rows, weight)
    table = jnp.concatenate([src_block, group_map, q_slot])
    mine, table = lax.optimization_barrier((mine, table))
    words = pack(mine, theirs)
    words = lax.all_to_all(words, ("near", "head"), 0, 0, tiled=True)
    words, scales = route(table, words)
    words = lax.all_to_all(words, "head", 0, 0, tiled=True)
    return opened(words, scales)


def solution(mesh):
    split = Mesh(mesh.devices.reshape(HEADS, 2, 2), ("head", "near", "core"))
    kdim = ("near", "core")
    return jax.shard_map(
        on_device,
        mesh=split,
        in_specs=(P(None, None, kdim), P(None, kdim, "head"), P(), P(), P()),
        out_specs=P(None, kdim, "head"),
        check_vma=False,
    )
```

time: 72.3 us -> 66.3 us (0.917)
  blocking collectives: 52.9 us -> 49.3 us
  Pallas kernels: 18.4 us -> 15.9 us
    pallas_call x5, Pallas kernels: 18.4 us -> 15.9 us  [the longest x1 5.97 us: away_product(): pl.pallas_call(away_kernel, in_specs=[HBM, HBM], out_specs=[VMEM, VMEM, V...]
    all_to_all x1, blocking collectives: 21 us -> 19 us  [on_device(): words = lax.all_to_all(words, 'head', 0, 0, tiled=True)]
    all_to_all x1, blocking collectives: 32 us -> 30.3 us  [on_device(): words = lax.all_to_all(words, ('near', 'head'), 0, 0, tiled=True)]
  transfers between devices with their start and end apart: 1 -> 1, of which waited for: 0 -> 1; matrix products, arithmetic and copies ran while one was open for 0% -> 0% of each run, Pallas kernels for 6% -> 6%
where the time goes in v3:
time: 66.3 us; the launch traced here: 66.1 us
  blocking collectives  49.3 us (74%)
  Pallas kernels  15.9 us (24%)
    all_to_all x1, blocking collectives, on_device(): words = lax.all_to_all(words, ('near', 'head'), 0, 0, tiled=True)  30.3 us
    all_to_all x1, blocking collectives, on_device(): words = lax.all_to_all(words, 'head', 0, 0, tiled=True)  19 us
    pallas_call x1, Pallas kernels, away_product(): pl.pallas_call(away_kernel, in_specs=[HBM, HBM], out_specs=[VMEM, VMEM, V...  5.97 us
    pallas_call x1, Pallas kernels, my_product(): pl.pallas_call(my_kernel, in_specs=[VMEM, VMEM], out_specs=VMEM, out_shap...  3.81 us
    pallas_call x1, Pallas kernels, route(): pl.pallas_call(route_kernel, in_specs=[SMEM, VMEM], out_specs=[VMEM, VMEM...  2.45 us
    pallas_call x1, Pallas kernels, opened(): pl.pallas_call(open_kernel, grid=(HEADS // OPEN_HEADS,), in_specs=[VMEM,...  1.99 us
    pallas_call x1, Pallas kernels, pack(): pl.pallas_call(pack_kernel, in_specs=[VMEM, VMEM], out_specs=VMEM, out_sh...  1.72 us
  transfers between devices with their start and end apart: 1, of which 1 were waited for; matrix products, arithmetic and copies ran while one was open for 0% of the time, Pallas kernels for 6%

profile of v3, /device:TPU:0, one launch (start us, length us, event | category | flops | bytes accessed | tf_op | source)
XLA Modules:
  0.0 66.1 jit_solution(2754164649219501928)
XLA Ops:
  0.0 0.0 copy-start
  0.0 0.0 copy-start.1
  0.0 0.0 copy-start.2
  0.0 6.0 %away_product.1 = (f32[3,512,384]{2,1,0:T(8,128)S(1)}, bf16[3,512,2048]{2,1,0:T(8,128)(2,1)S(1)}, bf16[3,384,2048]{2,1,0:T(8,128)(2,1)S(1)}) custom-call(bf16[3,1024,2048]{2,1,0:T(8,128)(2,1)} %hidden.1, bf16[3,320,2048]{2,1,0:T(8,128)(2,1)} %bitcast.1), custom_call_target="tpu_custom_call" | custom-call | flops 2415919104 | bytes 20000000 | tf_op jit(solution)/shard_map/away_product/pallas_call | solution.py:125
  6.0 0.1 collective-permute-start
  6.1 0.0 copy-done
  6.1 0.0 copy-done.1
  6.1 0.0 copy-done.2
  6.1 0.1 pad_add_fusion.table
  6.2 3.8 %my_product.1.mine = f32[3,512,384]{2,1,0:T(8,128)S(1)} custom-call(bf16[3,512,2048]{2,1,0:T(8,128)(2,1)S(1)} %get-tuple-element.12.rows, bf16[3,384,2048]{2,1,0:T(8,128)(2,1)S(1)} %get-tuple-element.13.weight), custom_call_target="tpu_custom_call" | custom-call | flops 2415919104 | bytes 12000000 | tf_op jit(solution)/shard_map/my_product/pallas_call | solution.py:153
  10.0 0.6 collective-permute-done.theirs
  10.6 1.7 %pack.1 = s32[64,32,128]{2,1,0:T(8,128)S(1)} custom-call(f32[3,512,384]{2,1,0:T(8,128)S(1)} %my_product.1.mine, f32[3,512,384]{2,1,0:T(8,128)S(1)} %collective-permute-done.theirs), custom_call_target="tpu_custom_call" | custom-call | tf_op jit(solution)/shard_map/pack/pallas_call | solution.py:215
  12.3 30.3 %all_to_all.10.words = s32[64,32,128]{2,1,0:T(8,128)S(1)} all-to-all(s32[64,32,128]{2,1,0:T(8,128)S(1)} %pack.1), channel_id=1, replica_groups=mesh['head'=32,'near'=2,'core'=2] {'near','head'}, dimensions={0} | all-to-all | bytes 2097152 | tf_op jit(solution)/shard_map/all_to_all | solution.py:356
  42.6 2.5 %route.1 = (s32[32,48,128]{2,1,0:T(8,128)S(1)}, f32[8,128]{1,0:T(8,128)S(1)}) custom-call(s32[80]{0:T(128)S(1)} %pad_add_fusion.table, s32[64,32,128]{2,1,0:T(8,128)S(1)} %all_to_all.10.words), custom_call_target="tpu_custom_call" | custom-call | tf_op jit(solution)/shard_map/route/pallas_call | solution.py:297
  45.1 19.0 %all_to_all.11.words = s32[32,48,128]{2,1,0:T(8,128)S(1)} all-to-all(s32[32,48,128]{2,1,0:T(8,128)S(1)} %get-tuple-element.17), channel_id=1, replica_groups=mesh['head'=32,'near'=2,'core'=2] {'head'}, dimensions={0} | all-to-all | bytes 1572864 | tf_op jit(solution)/shard_map/all_to_all | solution.py:358
  64.1 2.0 %opened.1 = f32[3,256,512]{2,1,0:T(8,128)} custom-call(s32[32,48,128]{2,1,0:T(8,128)S(1)} %all_to_all.11.words, f32[8,128]{1,0:T(8,128)S(1)} %get-tuple-element.18.scales), custom_call_target="tpu_custom_call" | custom-call | tf_op jit(solution)/shard_map/opened/pallas_call | solution.py:336
Async XLA Ops:
  0.0 6.1 %copy-start = (s32[64]{0:T(128)S(1)}, s32[64]{0:T(128)}, u32[]{:S(2)}) copy-start(s32[64]{0:T(128)} %param.9) | copy-start | bytes 772
  0.0 6.1 %copy-start.1 = (s32[8]{0:T(128)S(1)}, s32[8]{0:T(128)}, u32[]{:S(2)}) copy-start(s32[8]{0:T(128)} %param.8) | copy-start | bytes 100
  0.0 6.1 %copy-start.2 = (s32[8]{0:T(128)S(1)}, s32[8]{0:T(128)}, u32[]{:S(2)}) copy-start(s32[8]{0:T(128)} %param.7) | copy-start | bytes 100
  6.0 4.6 %collective-permute-start = (f32[3,512,384]{2,1,0:T(8,128)S(1)}, f32[3,512,384]{2,1,0:T(8,128)S(1)}, u32[]{:S(2)}, u32[]{:S(2)}) collective-permute-start(f32[3,512,384]{2,1,0:T(8,128)S(1)} %get-tuple-element.16), channel_id=1, source_target_pairs={{0,1},{1,0},{2,3},{3,2},{4,5},{5,4},{6,7},{7,6},{8,9},{9,8},{10,11... | collective-permute-start | bytes 7077896 | tf_op jit(solution)/shard_map/ppermute | solution.py:351

commit v4 on v3

--- a/solution.py
+++ b/solution.py
@@ -12,6 +12,7 @@
 LANES = 128
 WIDTH = 320
 PADDED = 384
+EARLY = 2
 HEADS = 32
 GROUP_DEVS = 4
 KV_HEADS = 8
@@ -101,7 +102,7 @@
             copy.start()
         for x in range(2):
             rows_copy(l, x, True).start()
-    for l in range(LAYERS):
+    for l in range(EARLY):
         for x in range(2):
             rows_copy(l, x, False).start()
     nothing = pl.multiple_of(320 - 64 * odd, 64)
@@ -116,7 +117,7 @@
             rows_copy(l, x, True).wait()
         out[l] = product_of(away_rows[l], weight_rows[l])
 
-    for l in range(LAYERS):
+    for l in range(EARLY):
         for x in range(2):
             rows_copy(l, x, False).wait()
 
@@ -132,7 +133,7 @@
         ],
         out_shape=[
             pltpu.VMEM((LAYERS, MINE, PADDED), jnp.float32),
-            pltpu.VMEM((LAYERS, MINE, DEPTH), jnp.bfloat16),
+            pltpu.VMEM((EARLY, MINE, DEPTH), jnp.bfloat16),
             pltpu.VMEM((LAYERS, PADDED, DEPTH), jnp.bfloat16),
         ],
         cost_estimate=pl.CostEstimate(
@@ -143,27 +144,56 @@
     )(hidden, weight)
 
 
-def my_kernel(rows, weight, out):
-    @pl.loop(0, LAYERS)
-    def _(l):
+def my_kernel(
+    hidden, rows, weight, src, grp, slot, out, src_out, grp_out, slot_out, late, arrived
+):
+    core = lax.axis_index("core")
+    copies = []
+    for x in range(2):
+        first = pl.multiple_of((2 * x + core) * SLICE, SLICE)
+        copies.append(
+            pltpu.make_async_copy(
+                hidden.at[EARLY, pl.ds(first, SLICE), :],
+                late.at[pl.ds(SLICE * x, SLICE), :],
+                arrived.at[x],
+            )
+        )
+    for k, (here, there) in enumerate(((src, src_out), (grp, grp_out), (slot, slot_out))):
+        copies.append(pltpu.make_async_copy(here, there, arrived.at[2 + k]))
+    for copy in copies:
+        copy.start()
+
+    for l in range(EARLY):
         out[l] = product_of(rows[l], weight[l])
-
-
-def my_product(rows, weight):
+    for copy in copies:
+        copy.wait()
+    out[EARLY] = product_of(late[...], weight[EARLY])
+
+
+def my_product(hidden, rows, weight, src_block, group_map, q_slot):
     return pl.pallas_call(
         my_kernel,
-        in_specs=[VMEM, VMEM],
-        out_specs=VMEM,
-        out_shape=pltpu.VMEM((LAYERS, MINE, PADDED), jnp.float32),
+        in_specs=[HBM, VMEM, VMEM, HBM, HBM, HBM],
+        out_specs=[VMEM, SMEM, SMEM, SMEM],
+        scratch_shapes=[
+            pltpu.VMEM((MINE, DEPTH), jnp.bfloat16),
+            pltpu.SemaphoreType.DMA((5,)),
+        ],
+        out_shape=[
+            pltpu.VMEM((LAYERS, MINE, PADDED), jnp.float32),
+            pltpu.SMEM((KV_HEADS,), jnp.int32),
+            pltpu.SMEM((KV_HEADS,), jnp.int32),
+            pltpu.SMEM((KV_HEADS * GROUP,), jnp.int32),
+        ],
         cost_estimate=pl.CostEstimate(
             flops=LAYERS * MINE * DEPTH * PADDED * 2, bytes_accessed=12_000_000, transcendentals=0
         ),
         compiler_params=limit(24),
         name="my_product",
-    )(rows, weight)
-
-
-PACK_UNROLL = 8
+    )(hidden, rows, weight, src_block, group_map, q_slot)
+
+
+PACK_UNROLL = 16
 
 
 def pack_kernel(mine, theirs, out):
@@ -222,7 +252,7 @@
     )(mine, theirs)
 
 
-def route_kernel(table, words, out, scales, whole_q, where_q):
+def route_kernel(src, grp, slot, words, out, scales, whole_q, where_q):
     reach = []
     for x in range(2):
         tops = []
@@ -238,12 +268,12 @@
     inverse = 1.0 / reach[:, 96:97]
     left = lanes() < 64
 
-    @pl.loop(0, KV_HEADS)
+    @pl.loop(0, KV_HEADS, unroll=True)
     def _(r):
-        source = table[r] * GROUP_DEVS
-        target = table[KV_HEADS + r] * GROUP_DEVS
+        source = src[r] * GROUP_DEVS
+        target = grp[r] * GROUP_DEVS
         for j in range(GROUP):
-            where_q[table[2 * KV_HEADS + r * GROUP + j]] = j
+            where_q[slot[r * GROUP + j]] = j
         blocks = [[None] * 10 for _ in range(LAYERS)]
         for pair in range(2):
             even, odd = 2 * pair, 2 * pair + 1
@@ -293,10 +323,10 @@
                 out[target + s, 8 * l : 8 * l + 8, :] = packed(whole_q[first, l], whole_q[second, l])
 
 
-def route(table, words):
+def route(src, grp, slot, words):
     return pl.pallas_call(
         route_kernel,
-        in_specs=[SMEM, VMEM],
+        in_specs=[SMEM, SMEM, SMEM, VMEM],
         out_specs=[VMEM, VMEM],
         scratch_shapes=[
             pltpu.VMEM((GROUP, LAYERS, 8, LANES), jnp.int32),
@@ -308,10 +338,10 @@
         ],
         compiler_params=limit(16),
         name="route",
-    )(table, words)
-
-
-OPEN_HEADS = 8
+    )(src, grp, slot, words)
+
+
+OPEN_HEADS = 16
 
 
 def open_kernel(words, scales, out):
@@ -349,12 +379,11 @@
     weight = pltpu.with_memory_space_constraint(jnp.swapaxes(joined_weight, 1, 2), pltpu.HBM)
     away, rows, weight = away_product(hidden, weight)
     theirs = lax.ppermute(away, "core", [(0, 1), (1, 0)])
-    mine = my_product(rows, weight)
-    table = jnp.concatenate([src_block, group_map, q_slot])
-    mine, table = lax.optimization_barrier((mine, table))
+    tables = [pltpu.with_memory_space_constraint(t, pltpu.HBM) for t in (src_block, group_map, q_slot)]
+    mine, *tables = my_product(hidden, rows, weight, *tables)
     words = pack(mine, theirs)
     words = lax.all_to_all(words, ("near", "head"), 0, 0, tiled=True)
-    words, scales = route(table, words)
+    words, scales = route(*tables, words)
     words = lax.all_to_all(words, "head", 0, 0, tiled=True)
     return opened(words, scales)
 

time: 66.3 us -> 64.2 us (0.968)
  Pallas kernels: 15.9 us -> 13.6 us
  blocking collectives: 49.3 us -> 50.2 us
    pallas_call x2, Pallas kernels: 6.26 us -> 5.3 us  [the longest x1 4.7 us: my_product(): pl.pallas_call(my_kernel, in_specs=[HBM, VMEM, VMEM, HBM, HBM, HBM], out_...]
    pallas_call x1, Pallas kernels: 1.99 us -> 1.33 us  [opened(): pl.pallas_call(open_kernel, grid=(HEADS // OPEN_HEADS,), in_specs=[VMEM,...]
  transfers between devices with their start and end apart: 1 -> 1, of which waited for: 1 -> 0; matrix products, arithmetic and copies ran while one was open for 0% -> 0% of each run, Pallas kernels for 6% -> 7%
where the time goes in v4:
time: 64.2 us; the launch traced here: 64 us
  blocking collectives  50.2 us (78%)
  Pallas kernels  13.6 us (21%)
    all_to_all x1, blocking collectives, on_device(): words = lax.all_to_all(words, ('near', 'head'), 0, 0, tiled=True)  30.7 us
    all_to_all x1, blocking collectives, on_device(): words = lax.all_to_all(words, 'head', 0, 0, tiled=True)  19.6 us
    pallas_call x1, Pallas kernels, away_product(): pl.pallas_call(away_kernel, in_specs=[HBM, HBM], out_specs=[VMEM, VMEM, V...  5.92 us
    pallas_call x1, Pallas kernels, my_product(): pl.pallas_call(my_kernel, in_specs=[HBM, VMEM, VMEM, HBM, HBM, HBM], out_...  4.7 us
    pallas_call x1, Pallas kernels, opened(): pl.pallas_call(open_kernel, grid=(HEADS // OPEN_HEADS,), in_specs=[VMEM,...  1.33 us
  transfers between devices with their start and end apart: 1, of which 0 were waited for; matrix products, arithmetic and copies ran while one was open for 0% of the time, Pallas kernels for 7%

profile of v4, /device:TPU:0, one launch (start us, length us, event | category | flops | bytes accessed | tf_op | source)
XLA Modules:
  0.0 64.0 jit_solution(13813769088501411087)
XLA Ops:
  0.0 5.9 %away_product.1 = (f32[3,512,384]{2,1,0:T(8,128)S(1)}, bf16[2,512,2048]{2,1,0:T(8,128)(2,1)S(1)}, bf16[3,384,2048]{2,1,0:T(8,128)(2,1)S(1)}) custom-call(bf16[3,1024,2048]{2,1,0:T(8,128)(2,1)} %hidden.3, bf16[3,320,2048]{2,1,0:T(8,128)(2,1)} %bitcast.1), custom_call_target="tpu_custom_call" | custom-call | flops 2415919104 | bytes 20000000 | tf_op jit(solution)/shard_map/away_product/pallas_call | solution.py:126
  5.9 0.1 collective-permute-start
  6.0 4.7 %my_product.1 = (f32[3,512,384]{2,1,0:T(8,128)S(1)}, s32[8]{0:T(128)S(4)}, s32[8]{0:T(128)S(4)}, s32[64]{0:T(128)S(4)}) custom-call(bf16[3,1024,2048]{2,1,0:T(8,128)(2,1)} %hidden.3, bf16[2,512,2048]{2,1,0:T(8,128)(2,1)S(1)} %get-tuple-element.14.rows, bf16[3,384,2048]{2,1,0:T(8,128)(2,1)S(1)} %get-tuple-element.15.weight, s32[8]{0:T(128)} %src.1, s32[8]{0:T(128)} %grp.1, ...), custom_call_target="tpu_custom_call" | custom-call | flops 2415919104 | bytes 12000000 | tf_op jit(solution)/shard_map/my_product/pallas_call | solution.py:174
  10.7 0.0 collective-permute-done.theirs
  10.7 1.1 %pack.1 = s32[64,32,128]{2,1,0:T(8,128)S(1)} custom-call(f32[3,512,384]{2,1,0:T(8,128)S(1)} %get-tuple-element.19.mine, f32[3,512,384]{2,1,0:T(8,128)S(1)} %collective-permute-done.theirs), custom_call_target="tpu_custom_call" | custom-call | tf_op jit(solution)/shard_map/pack/pallas_call | solution.py:245
  11.8 30.7 %all_to_all.10.words = s32[64,32,128]{2,1,0:T(8,128)S(1)} all-to-all(s32[64,32,128]{2,1,0:T(8,128)S(1)} %pack.1), channel_id=1, replica_groups=mesh['head'=32,'near'=2,'core'=2] {'near','head'}, dimensions={0} | all-to-all | bytes 2097152 | tf_op jit(solution)/shard_map/all_to_all | solution.py:385
  42.5 0.6 route.1
  43.1 19.6 %all_to_all.11.words = s32[32,48,128]{2,1,0:T(8,128)S(1)} all-to-all(s32[32,48,128]{2,1,0:T(8,128)S(1)} %get-tuple-element.21), channel_id=1, replica_groups=mesh['head'=32,'near'=2,'core'=2] {'head'}, dimensions={0} | all-to-all | bytes 1572864 | tf_op jit(solution)/shard_map/all_to_all | solution.py:387
  62.7 1.3 %opened.1 = f32[3,256,512]{2,1,0:T(8,128)} custom-call(s32[32,48,128]{2,1,0:T(8,128)S(1)} %all_to_all.11.words, f32[8,128]{1,0:T(8,128)S(1)} %get-tuple-element.22.scales), custom_call_target="tpu_custom_call" | custom-call | tf_op jit(solution)/shard_map/opened/pallas_call | solution.py:366
Async XLA Ops:
  5.9 4.8 %collective-permute-start = (f32[3,512,384]{2,1,0:T(8,128)S(1)}, f32[3,512,384]{2,1,0:T(8,128)S(1)}, u32[]{:S(2)}, u32[]{:S(2)}) collective-permute-start(f32[3,512,384]{2,1,0:T(8,128)S(1)} %get-tuple-element.20), channel_id=1, source_target_pairs={{0,1},{1,0},{2,3},{3,2},{4,5},{5,4},{6,7},{7,6},{8,9},{9,8},{10,11... | collective-permute-start | bytes 7077896 | tf_op jit(solution)/shard_map/ppermute | solution.py:381

commit v5 on v4

--- a/solution.py
+++ b/solution.py
@@ -11,7 +11,6 @@
 DEPTH = 2048
 LANES = 128
 WIDTH = 320
-PADDED = 384
 EARLY = 2
 HEADS = 32
 GROUP_DEVS = 4
@@ -63,7 +62,7 @@
 
 def product_of(rows, weight):
     return lax.dot_general(
-        rows, weight, (((1,), (1,)), ((), ())), preferred_element_type=jnp.float32
+        weight, rows, (((1,), (1,)), ((), ())), preferred_element_type=jnp.float32
     )
 
 
@@ -83,7 +82,6 @@
     def weight_copies(l):
         blocks = pl.multiple_of(64 * odd, 64)
         half = pl.multiple_of(256 * (1 - odd), 64)
-        place = pl.multiple_of(256 + 64 * odd, 64)
         return [
             pltpu.make_async_copy(
                 weight.at[l, pl.ds(blocks, 256), :],
@@ -92,7 +90,7 @@
             ),
             pltpu.make_async_copy(
                 weight.at[l, pl.ds(half, 64), :],
-                weight_rows.at[l, pl.ds(place, 64), :],
+                weight_rows.at[l, pl.ds(256, 64), :],
                 arrived.at[l, 5],
             ),
         ]
@@ -105,9 +103,6 @@
     for l in range(EARLY):
         for x in range(2):
             rows_copy(l, x, False).start()
-    nothing = pl.multiple_of(320 - 64 * odd, 64)
-    for l in range(LAYERS):
-        weight_rows[l, pl.ds(nothing, 64), :] = jnp.zeros((64, DEPTH), jnp.bfloat16)
 
     @pl.loop(0, LAYERS)
     def _(l):
@@ -132,12 +127,12 @@
             pltpu.SemaphoreType.DMA((LAYERS, 6)),
         ],
         out_shape=[
-            pltpu.VMEM((LAYERS, MINE, PADDED), jnp.float32),
+            pltpu.VMEM((LAYERS, WIDTH, MINE), jnp.float32),
             pltpu.VMEM((EARLY, MINE, DEPTH), jnp.bfloat16),
-            pltpu.VMEM((LAYERS, PADDED, DEPTH), jnp.bfloat16),
+            pltpu.VMEM((LAYERS, WIDTH, DEPTH), jnp.bfloat16),
         ],
         cost_estimate=pl.CostEstimate(
-            flops=LAYERS * MINE * DEPTH * PADDED * 2, bytes_accessed=20_000_000, transcendentals=0
+            flops=LAYERS * MINE * DEPTH * WIDTH * 2, bytes_accessed=20_000_000, transcendentals=0
         ),
         compiler_params=limit(44),
         name="away_product",
@@ -163,8 +158,10 @@
     for copy in copies:
         copy.start()
 
-    for l in range(EARLY):
+    @pl.loop(0, EARLY)
+    def _(l):
         out[l] = product_of(rows[l], weight[l])
+
     for copy in copies:
         copy.wait()
     out[EARLY] = product_of(late[...], weight[EARLY])
@@ -180,65 +177,70 @@
             pltpu.SemaphoreType.DMA((5,)),
         ],
         out_shape=[
-            pltpu.VMEM((LAYERS, MINE, PADDED), jnp.float32),
+            pltpu.VMEM((LAYERS, WIDTH, MINE), jnp.float32),
             pltpu.SMEM((KV_HEADS,), jnp.int32),
             pltpu.SMEM((KV_HEADS,), jnp.int32),
             pltpu.SMEM((KV_HEADS * GROUP,), jnp.int32),
         ],
         cost_estimate=pl.CostEstimate(
-            flops=LAYERS * MINE * DEPTH * PADDED * 2, bytes_accessed=12_000_000, transcendentals=0
+            flops=LAYERS * MINE * DEPTH * WIDTH * 2, bytes_accessed=12_000_000, transcendentals=0
         ),
         compiler_params=limit(24),
         name="my_product",
     )(hidden, rows, weight, src_block, group_map, q_slot)
 
 
-PACK_UNROLL = 16
+TILES = LANES // 8
 
 
 def pack_kernel(mine, theirs, out):
     lane = lanes()
     odd = lax.axis_index("head") & 1
-    spare = (lane >= 64) != (odd == 1)
+    is_odd = odd == 1
+    spare = (lane >= 64) != is_odd
     slot = lane & 63
-    for x in range(2):
-
-        def pack_tiles(step, codes):
-            for i in range(PACK_UNROLL):
-                head = step * PACK_UNROLL + i
-                block = x * HEADS + head
-                rows = pl.ds(pl.multiple_of(8 * block, 8), 8)
-                tiles = [mine[l, rows, :] + theirs[l, rows, :] for l in range(LAYERS)]
-                top = jnp.maximum(
-                    jnp.maximum(jnp.abs(tiles[0]), jnp.abs(tiles[1])), jnp.abs(tiles[2])
-                )
-                code = codes_of(jnp.max(top, axis=1, keepdims=True))
-                inverse = inverse_scale_of(code)
-                rest = []
-                for l in range(LAYERS):
-                    a, b, c = [
-                        whole(tiles[l][:, LANES * t : LANES * t + LANES] * inverse)
-                        for t in range(3)
-                    ]
-                    out[block, 8 * l : 8 * l + 8, :] = packed(a, b)
-                    rest.append(c)
-                low = rest[0] + pltpu.roll(rest[1], 64, 1)
-                out[block, 24:32, :] = packed(low, jnp.where(spare, code, rest[2]))
-                codes = jnp.where(slot == head, code, codes)
-            return codes
-
-        codes = lax.fori_loop(
-            0, HEADS // PACK_UNROLL, pack_tiles, jnp.zeros((8, LANES), jnp.int32)
-        )
-        codes = codes << 16
+
+    @pl.loop(0, 2)
+    def _(x):
+        codes = jnp.zeros((8, LANES), jnp.int32)
+        for j in range(SLICE // LANES):
+            tokens = pl.ds(pl.multiple_of(x * SLICE + j * LANES, LANES), LANES)
+
+            def sums(l, first, size):
+                rows = pl.ds(first, size)
+                return mine[l, rows, tokens] + theirs[l, rows, tokens]
+
+            top = None
+            for l in range(LAYERS):
+                for first in range(0, WIDTH, 8):
+                    value = jnp.abs(sums(l, first, 8))
+                    top = value if top is None else jnp.maximum(top, value)
+            code = codes_of(jnp.max(top, axis=0, keepdims=True))
+            inverse = inverse_scale_of(code)
+            first_tile = x * HEADS + j * TILES
+            rest = []
+            for l in range(LAYERS):
+                a = whole(sums(l, 0, LANES) * inverse)
+                b = whole(sums(l, LANES, LANES) * inverse)
+                words = packed(a, b).T.reshape(TILES, 8, LANES)
+                out[pl.ds(first_tile, TILES), 8 * l : 8 * l + 8, :] = words
+                rest.append(whole(sums(l, 2 * LANES, 64) * inverse))
+            shown = jnp.broadcast_to(code, (64, LANES))
+            low = jnp.concatenate(
+                [jnp.where(is_odd, rest[1], rest[0]), jnp.where(is_odd, rest[0], rest[1])], axis=0
+            )
+            high = jnp.concatenate(
+                [jnp.where(is_odd, shown, rest[2]), jnp.where(is_odd, rest[2], shown)], axis=0
+            )
+            words = packed(low, high).T.reshape(TILES, 8, LANES)
+            out[pl.ds(first_tile, TILES), 24:32, :] = words
+            for i in range(TILES):
+                codes = jnp.where(slot == j * TILES + i, words[i], codes)
+        codes = codes & ~0xFFFF
         shown = spare & (slot < HEADS)
-
-        @pl.loop(0, HEADS // PACK_UNROLL)
-        def _(step):
-            for i in range(PACK_UNROLL):
-                block = x * HEADS + step * PACK_UNROLL + i
-                word = out[block, 24:32, :]
-                out[block, 24:32, :] = jnp.where(shown, (word & 0xFFFF) | codes, word)
+        for i in range(HEADS):
+            word = out[x * HEADS + i, 24:32, :]
+            out[x * HEADS + i, 24:32, :] = jnp.where(shown, (word & 0xFFFF) | codes, word)
 
 
 def pack(mine, theirs):

time: 64.2 us -> 61.8 us (0.963)
  Pallas kernels: 13.6 us -> 11 us
  waiting for transfers between devices: 0.01 us -> 1.23 us
  blocking collectives: 50.2 us -> 49.3 us
    pallas_call x1, Pallas kernels: 4.7 us -> 2.72 us  [my_product(): pl.pallas_call(my_kernel, in_specs=[HBM, VMEM, VMEM, HBM, HBM, HBM], out_...]
    ppermute x1, waiting for transfers between devices: 0.01 us -> 1.23 us  [on_device(): theirs = lax.ppermute(away, 'core', [(0, 1), (1, 0)])]
    pallas_call x1, Pallas kernels: 5.92 us -> 5.27 us  [away_product(): pl.pallas_call(away_kernel, in_specs=[HBM, HBM], out_specs=[VMEM, VMEM, V...]
  transfers between devices with their start and end apart: 1 -> 1, of which waited for: 0 -> 1; matrix products, arithmetic and copies ran while one was open for 0% -> 0% of each run, Pallas kernels for 7% -> 4%
where the time goes in v5:
time: 61.8 us; the launch traced here: 61.7 us
  blocking collectives  49.3 us (80%)
  Pallas kernels  11 us (18%)
  waiting for transfers between devices  1.23 us (2%)
    all_to_all x1, blocking collectives, on_device(): words = lax.all_to_all(words, ('near', 'head'), 0, 0, tiled=True)  30.3 us
    all_to_all x1, blocking collectives, on_device(): words = lax.all_to_all(words, 'head', 0, 0, tiled=True)  19 us
    pallas_call x1, Pallas kernels, away_product(): pl.pallas_call(away_kernel, in_specs=[HBM, HBM], out_specs=[VMEM, VMEM, V...  5.27 us
    pallas_call x1, Pallas kernels, my_product(): pl.pallas_call(my_kernel, in_specs=[HBM, VMEM, VMEM, HBM, HBM, HBM], out_...  2.72 us
    pallas_call x1, Pallas kernels, opened(): pl.pallas_call(open_kernel, grid=(HEADS // OPEN_HEADS,), in_specs=[VMEM,...  1.33 us
  transfers between devices with their start and end apart: 1, of which 1 were waited for; matrix products, arithmetic and copies ran while one was open for 0% of the time, Pallas kernels for 4%

profile of v5, /device:TPU:0, one launch (start us, length us, event | category | flops | bytes accessed | tf_op | source)
XLA Modules:
  0.0 61.7 jit_solution(5036557769662789000)
XLA Ops:
  0.0 5.3 %away_product.1 = (f32[3,320,512]{2,1,0:T(8,128)S(1)}, bf16[2,512,2048]{2,1,0:T(8,128)(2,1)S(1)}, bf16[3,320,2048]{2,1,0:T(8,128)(2,1)S(1)}) custom-call(bf16[3,1024,2048]{2,1,0:T(8,128)(2,1)} %hidden.3, bf16[3,320,2048]{2,1,0:T(8,128)(2,1)} %bitcast.1), custom_call_target="tpu_custom_call" | custom-call | flops 2013265920 | bytes 20000000 | tf_op jit(solution)/shard_map/away_product/pallas_call | solution.py:121
  5.3 0.1 collective-permute-start
  5.4 2.7 %my_product.1 = (f32[3,320,512]{2,1,0:T(8,128)S(1)}, s32[8]{0:T(128)S(4)}, s32[8]{0:T(128)S(4)}, s32[64]{0:T(128)S(4)}) custom-call(bf16[3,1024,2048]{2,1,0:T(8,128)(2,1)} %hidden.3, bf16[2,512,2048]{2,1,0:T(8,128)(2,1)S(1)} %get-tuple-element.14.rows, bf16[3,320,2048]{2,1,0:T(8,128)(2,1)S(1)} %get-tuple-element.15.weight, s32[8]{0:T(128)} %src.1, s32[8]{0:T(128)} %grp.1, ...), custom_call_target="tpu_custom_call" | custom-call | flops 2013265920 | bytes 12000000 | tf_op jit(solution)/shard_map/my_product/pallas_call | solution.py:171
  8.1 1.2 %collective-permute-done.theirs = f32[3,320,512]{2,1,0:T(8,128)S(1)} collective-permute-done((f32[3,320,512]{2,1,0:T(8,128)S(1)}, f32[3,320,512]{2,1,0:T(8,128)S(1)}, u32[]{:S(2)}, u32[]{:S(2)}) %collective-permute-start) | collective-permute-done | bytes 1966112 | tf_op jit(solution)/shard_map/ppermute | solution.py:383
  9.3 1.1 %pack.1 = s32[64,32,128]{2,1,0:T(8,128)S(1)} custom-call(f32[3,320,512]{2,1,0:T(8,128)S(1)} %get-tuple-element.19.mine, f32[3,320,512]{2,1,0:T(8,128)S(1)} %collective-permute-done.theirs), custom_call_target="tpu_custom_call" | custom-call | tf_op jit(solution)/shard_map/pack/pallas_call | solution.py:247
  10.4 30.3 %all_to_all.10.words = s32[64,32,128]{2,1,0:T(8,128)S(1)} all-to-all(s32[64,32,128]{2,1,0:T(8,128)S(1)} %pack.1), channel_id=1, replica_groups=mesh['head'=32,'near'=2,'core'=2] {'near','head'}, dimensions={0} | all-to-all | bytes 2097152 | tf_op jit(solution)/shard_map/all_to_all | solution.py:387
  40.7 0.6 route.1
  41.3 19.0 %all_to_all.11.words = s32[32,48,128]{2,1,0:T(8,128)S(1)} all-to-all(s32[32,48,128]{2,1,0:T(8,128)S(1)} %get-tuple-element.21), channel_id=1, replica_groups=mesh['head'=32,'near'=2,'core'=2] {'head'}, dimensions={0} | all-to-all | bytes 1572864 | tf_op jit(solution)/shard_map/all_to_all | solution.py:389
  60.3 1.3 %opened.1 = f32[3,256,512]{2,1,0:T(8,128)} custom-call(s32[32,48,128]{2,1,0:T(8,128)S(1)} %all_to_all.11.words, f32[8,128]{1,0:T(8,128)S(1)} %get-tuple-element.22.scales), custom_call_target="tpu_custom_call" | custom-call | tf_op jit(solution)/shard_map/opened/pallas_call | solution.py:368
Async XLA Ops:
  5.3 4.1 %collective-permute-start = (f32[3,320,512]{2,1,0:T(8,128)S(1)}, f32[3,320,512]{2,1,0:T(8,128)S(1)}, u32[]{:S(2)}, u32[]{:S(2)}) collective-permute-start(f32[3,320,512]{2,1,0:T(8,128)S(1)} %get-tuple-element.20), channel_id=1, source_target_pairs={{0,1},{1,0},{2,3},{3,2},{4,5},{5,4},{6,7},{7,6},{8,9},{9,8},{10,11... | collective-permute-start | bytes 5898248 | tf_op jit(solution)/shard_map/ppermute | solution.py:383

commit v6 on v5

--- a/solution.py
+++ b/solution.py
@@ -11,6 +11,7 @@
 DEPTH = 2048
 LANES = 128
 WIDTH = 320
+CODE_ROW = 160
 EARLY = 2
 HEADS = 32
 GROUP_DEVS = 4
@@ -56,6 +57,10 @@
     return words >> 16
 
 
+def column_of(head):
+    return ((head >> 1) & 3) * 4 + (head >> 3)
+
+
 def lanes():
     return lax.broadcasted_iota(jnp.int32, (8, LANES), 1)
 
@@ -68,7 +73,7 @@
 
 def away_kernel(hidden, weight, out, my_rows, weight_rows, away_rows, arrived):
     core = lax.axis_index("core")
-    odd = lax.axis_index("head") & 1
+    odd = lax.axis_index("far")
 
     def rows_copy(l, x, other):
         first = pl.multiple_of((2 * x + (1 - core if other else core)) * SLICE, SLICE)
@@ -110,7 +115,12 @@
             copy.wait()
         for x in range(2):
             rows_copy(l, x, True).wait()
-        out[l] = product_of(away_rows[l], weight_rows[l])
+        value = product_of(away_rows[l], weight_rows[l])
+        code = codes_of(jnp.max(jnp.abs(value), axis=0, keepdims=True))
+        value = whole(value * inverse_scale_of(code))
+        out[l, :LANES, :] = packed(value[:LANES], value[LANES : 2 * LANES])
+        out[l, LANES:CODE_ROW, :] = packed(value[2 * LANES : 2 * LANES + 32], value[2 * LANES + 32 :])
+        out[l, CODE_ROW:, :] = jnp.broadcast_to(code, (8, MINE))
 
     for l in range(EARLY):
         for x in range(2):
@@ -127,7 +137,7 @@
             pltpu.SemaphoreType.DMA((LAYERS, 6)),
         ],
         out_shape=[
-            pltpu.VMEM((LAYERS, WIDTH, MINE), jnp.float32),
+            pltpu.VMEM((LAYERS, CODE_ROW + 8, MINE), jnp.int32),
             pltpu.VMEM((EARLY, MINE, DEPTH), jnp.bfloat16),
             pltpu.VMEM((LAYERS, WIDTH, DEPTH), jnp.bfloat16),
         ],
@@ -193,9 +203,9 @@
 TILES = LANES // 8
 
 
-def pack_kernel(mine, theirs, out):
+def pack_kernel(mine, theirs, out, sums):
     lane = lanes()
-    odd = lax.axis_index("head") & 1
+    odd = lax.axis_index("far")
     is_odd = odd == 1
     spare = (lane >= 64) != is_odd
     slot = lane & 63
@@ -203,28 +213,36 @@
     @pl.loop(0, 2)
     def _(x):
         codes = jnp.zeros((8, LANES), jnp.int32)
+        first = x * (HEADS // 2)
+
+        def place(head):
+            return (head & 1) * HEADS + column_of(head)
+
         for j in range(SLICE // LANES):
             tokens = pl.ds(pl.multiple_of(x * SLICE + j * LANES, LANES), LANES)
 
-            def sums(l, first, size):
-                rows = pl.ds(first, size)
-                return mine[l, rows, tokens] + theirs[l, rows, tokens]
-
             top = None
             for l in range(LAYERS):
-                for first in range(0, WIDTH, 8):
-                    value = jnp.abs(sums(l, first, 8))
-                    top = value if top is None else jnp.maximum(top, value)
+                scale = scale_of(theirs[l, CODE_ROW:, tokens])
+                for at in range(0, CODE_ROW, 8):
+                    word = theirs[l, at : at + 8, tokens]
+                    low_row = at if at < LANES else at + LANES
+                    high_row = low_row + (LANES if at < LANES else 32)
+                    for row, half in ((low_row, low_of(word)), (high_row, high_of(word))):
+                        value = mine[l, row : row + 8, tokens] + half.astype(jnp.float32) * scale
+                        sums[l, row : row + 8, :] = value
+                        value = jnp.abs(value)
+                        top = value if top is None else jnp.maximum(top, value)
             code = codes_of(jnp.max(top, axis=0, keepdims=True))
             inverse = inverse_scale_of(code)
-            first_tile = x * HEADS + j * TILES
             rest = []
             for l in range(LAYERS):
-                a = whole(sums(l, 0, LANES) * inverse)
-                b = whole(sums(l, LANES, LANES) * inverse)
+                a = whole(sums[l, :LANES, :] * inverse)
+                b = whole(sums[l, LANES : 2 * LANES, :] * inverse)
                 words = packed(a, b).T.reshape(TILES, 8, LANES)
-                out[pl.ds(first_tile, TILES), 8 * l : 8 * l + 8, :] = words
-                rest.append(whole(sums(l, 2 * LANES, 64) * inverse))
+                for i in range(TILES):
+                    out[first + place(j * TILES + i), 8 * l : 8 * l + 8, :] = words[i]
+                rest.append(whole(sums[l, 2 * LANES :, :] * inverse))
             shown = jnp.broadcast_to(code, (64, LANES))
             low = jnp.concatenate(
                 [jnp.where(is_odd, rest[1], rest[0]), jnp.where(is_odd, rest[0], rest[1])], axis=0
@@ -233,14 +251,14 @@
                 [jnp.where(is_odd, shown, rest[2]), jnp.where(is_odd, rest[2], shown)], axis=0
             )
             words = packed(low, high).T.reshape(TILES, 8, LANES)
-            out[pl.ds(first_tile, TILES), 24:32, :] = words
             for i in range(TILES):
+                out[first + place(j * TILES + i), 24:32, :] = words[i]
                 codes = jnp.where(slot == j * TILES + i, words[i], codes)
         codes = codes & ~0xFFFF
         shown = spare & (slot < HEADS)
         for i in range(HEADS):
-            word = out[x * HEADS + i, 24:32, :]
-            out[x * HEADS + i, 24:32, :] = jnp.where(shown, (word & 0xFFFF) | codes, word)
+            word = out[first + place(i), 24:32, :]
+            out[first + place(i), 24:32, :] = jnp.where(shown, (word & 0xFFFF) | codes, word)
 
 
 def pack(mine, theirs):
@@ -248,6 +266,7 @@
         pack_kernel,
         in_specs=[VMEM, VMEM],
         out_specs=VMEM,
+        scratch_shapes=[pltpu.VMEM((LAYERS, WIDTH, LANES), jnp.float32)],
         out_shape=pltpu.VMEM((2 * HEADS, 32, LANES), jnp.int32),
         compiler_params=limit(16),
         name="pack",
@@ -260,8 +279,8 @@
         tops = []
         for parity in range(2):
             top = None
-            for m in range(parity, HEADS, 2):
-                code = high_of(words[x * HEADS + m, 24:32, :])
+            for m in range(HEADS // 2):
+                code = high_of(words[parity * HEADS + x * (HEADS // 2) + m, 24:32, :])
                 top = code if top is None else jnp.maximum(top, code)
             tops.append(top)
         reach.append(scale_of(jnp.maximum(tops[0], pltpu.roll(tops[1], 64, 1))))
@@ -272,8 +291,8 @@
 
     @pl.loop(0, KV_HEADS, unroll=True)
     def _(r):
-        source = src[r] * GROUP_DEVS
-        target = grp[r] * GROUP_DEVS
+        source = column_of(src[r] * GROUP_DEVS)
+        target = column_of(grp[r] * GROUP_DEVS)
         for j in range(GROUP):
             where_q[slot[r * GROUP + j]] = j
         blocks = [[None] * 10 for _ in range(LAYERS)]
@@ -284,7 +303,7 @@
             for x in range(2):
                 third = {}
                 for m in (even, odd):
-                    device = x * HEADS + source + m
+                    device = (m & 1) * HEADS + x * (HEADS // 2) + source + column_of(m)
                     last = words[device, 24:32, :]
                     low, high = low_of(last), high_of(last)
                     at = 96 if m == even else 32
@@ -318,11 +337,13 @@
                 whole_q[j, l] = whole(blocks[l][j])
             key_value = packed(whole(blocks[l][8]), whole(blocks[l][9]))
             for s in range(GROUP_DEVS):
-                out[target + s, 24 + 8 * l : 32 + 8 * l, :] = key_value
+                device = target + (s & 1) * (HEADS // 2) + column_of(s)
+                out[device, 24 + 8 * l : 32 + 8 * l, :] = key_value
         for s in range(GROUP_DEVS):
+            device = target + (s & 1) * (HEADS // 2) + column_of(s)
             first, second = where_q[2 * s] & 7, where_q[2 * s + 1] & 7
             for l in range(LAYERS):
-                out[target + s, 8 * l : 8 * l + 8, :] = packed(whole_q[first, l], whole_q[second, l])
+                out[device, 8 * l : 8 * l + 8, :] = packed(whole_q[first, l], whole_q[second, l])
 
 
 def route(src, grp, slot, words):
@@ -350,7 +371,7 @@
     step = pl.program_id(0)
     scale_columns = pltpu.roll(scales[...], 64 - OPEN_HEADS * step, 1)
     for i in range(OPEN_HEADS):
-        block = step * OPEN_HEADS + i
+        block = (i & 1) * (HEADS // 2) + column_of(i) + step * (OPEN_HEADS // 8)
         scale = scale_columns[:, i : i + 1]
         rows = slice(8 * i, 8 * i + 8)
         for l in range(LAYERS):
@@ -384,19 +405,19 @@
     tables = [pltpu.with_memory_space_constraint(t, pltpu.HBM) for t in (src_block, group_map, q_slot)]
     mine, *tables = my_product(hidden, rows, weight, *tables)
     words = pack(mine, theirs)
-    words = lax.all_to_all(words, ("near", "head"), 0, 0, tiled=True)
+    words = lax.all_to_all(words, ("far", "near", "y", "z"), 0, 0, tiled=True)
     words, scales = route(*tables, words)
-    words = lax.all_to_all(words, "head", 0, 0, tiled=True)
+    words = lax.all_to_all(words, ("far", "y", "z"), 0, 0, tiled=True)
     return opened(words, scales)
 
 
 def solution(mesh):
-    split = Mesh(mesh.devices.reshape(HEADS, 2, 2), ("head", "near", "core"))
-    kdim = ("near", "core")
+    split = Mesh(mesh.devices.reshape(4, 4, 2, 2, 2), ("z", "y", "far", "near", "core"))
+    head, kdim = ("z", "y", "far"), ("near", "core")
     return jax.shard_map(
         on_device,
         mesh=split,
-        in_specs=(P(None, None, kdim), P(None, kdim, "head"), P(), P(), P()),
-        out_specs=P(None, kdim, "head"),
+        in_specs=(P(None, None, kdim), P(None, kdim, head), P(), P(), P()),
+        out_specs=P(None, kdim, head),
         check_vma=False,
     )

time: 61.8 us -> 60.2 us (0.974)
  waiting for transfers between devices: 1.23 us -> 0.01 us
    ppermute x1, waiting for transfers between devices: 1.23 us -> 0.01 us  [on_device(): theirs = lax.ppermute(away, 'core', [(0, 1), (1, 0)])]
  transfers between devices with their start and end apart: 1 -> 1, of which waited for: 1 -> 0; matrix products, arithmetic and copies ran while one was open for 0% -> 0% of each run, Pallas kernels for 4% -> 5%
where the time goes in v6:
time: 60.2 us; the launch traced here: 60.1 us
  blocking collectives  49.2 us (82%)
  Pallas kernels  10.8 us (18%)
    all_to_all x1, blocking collectives, on_device(): words = lax.all_to_all(words, ('far', 'near', 'y', 'z'), 0, 0, tiled=True)  30.5 us
    all_to_all x1, blocking collectives, on_device(): words = lax.all_to_all(words, ('far', 'y', 'z'), 0, 0, tiled=True)  18.7 us
    pallas_call x1, Pallas kernels, away_product(): pl.pallas_call(away_kernel, in_specs=[HBM, HBM], out_specs=[VMEM, VMEM, V...  5.27 us
    pallas_call x1, Pallas kernels, my_product(): pl.pallas_call(my_kernel, in_specs=[HBM, VMEM, VMEM, HBM, HBM, HBM], out_...  2.72 us
    pallas_call x1, Pallas kernels, opened(): pl.pallas_call(open_kernel, grid=(HEADS // OPEN_HEADS,), in_specs=[VMEM,...  1.33 us
  transfers between devices with their start and end apart: 1, of which 0 were waited for; matrix products, arithmetic and copies ran while one was open for 0% of the time, Pallas kernels for 5%

profile of v6, /device:TPU:0, one launch (start us, length us, event | category | flops | bytes accessed | tf_op | source)
XLA Modules:
  0.0 60.1 jit_solution(2636646527843784925)
XLA Ops:
  0.0 5.3 %away_product.1 = (s32[3,168,512]{2,1,0:T(8,128)S(1)}, bf16[2,512,2048]{2,1,0:T(8,128)(2,1)S(1)}, bf16[3,320,2048]{2,1,0:T(8,128)(2,1)S(1)}) custom-call(bf16[3,1024,2048]{2,1,0:T(8,128)(2,1)} %hidden.3, bf16[3,320,2048]{2,1,0:T(8,128)(2,1)} %bitcast.1), custom_call_target="tpu_custom_call" | custom-call | flops 2013265920 | bytes 20000000 | tf_op jit(solution)/shard_map/away_product/pallas_call | solution.py:131
  5.3 0.1 collective-permute-start
  5.4 2.7 %my_product.1 = (f32[3,320,512]{2,1,0:T(8,128)S(1)}, s32[8]{0:T(128)S(4)}, s32[8]{0:T(128)S(4)}, s32[64]{0:T(128)S(4)}) custom-call(bf16[3,1024,2048]{2,1,0:T(8,128)(2,1)} %hidden.3, bf16[2,512,2048]{2,1,0:T(8,128)(2,1)S(1)} %get-tuple-element.14.rows, bf16[3,320,2048]{2,1,0:T(8,128)(2,1)S(1)} %get-tuple-element.15.weight, s32[8]{0:T(128)} %src.1, s32[8]{0:T(128)} %grp.1, ...), custom_call_target="tpu_custom_call" | custom-call | flops 2013265920 | bytes 12000000 | tf_op jit(solution)/shard_map/my_product/pallas_call | solution.py:181
  8.1 0.0 collective-permute-done.theirs
  8.1 0.9 %pack.1 = s32[64,32,128]{2,1,0:T(8,128)S(1)} custom-call(f32[3,320,512]{2,1,0:T(8,128)S(1)} %get-tuple-element.19.mine, s32[3,168,512]{2,1,0:T(8,128)S(1)} %collective-permute-done.theirs), custom_call_target="tpu_custom_call" | custom-call | tf_op jit(solution)/shard_map/pack/pallas_call | solution.py:265
  9.0 30.5 %all_to_all.10.words = s32[64,32,128]{2,1,0:T(8,128)S(1)} all-to-all(s32[64,32,128]{2,1,0:T(8,128)S(1)} %pack.1), channel_id=1, replica_groups=mesh['z'=4,'y'=4,'far'=2,'near'=2,'core'=2] {'far','near','y','z'}, dimensions={0} | all-to-all | bytes 2097152 | tf_op jit(solution)/shard_map/all_to_all | solution.py:408
  39.5 0.6 %route.1 = (s32[32,48,128]{2,1,0:T(8,128)S(1)}, f32[8,128]{1,0:T(8,128)S(1)}) custom-call(s32[8]{0:T(128)S(4)} %get-tuple-element.16.src, s32[8]{0:T(128)S(4)} %get-tuple-element.17.grp, s32[64]{0:T(128)S(4)} %get-tuple-element.18.slot, s32[64,32,128]{2,1,0:T(8,128)S(1)} %all_to_all.10.words), custom_call_target="tpu_custom_call" | custom-call | tf_op jit(solution)/shard_map/route/pallas_call | solution.py:350
  40.1 18.7 %all_to_all.11.words = s32[32,48,128]{2,1,0:T(8,128)S(1)} all-to-all(s32[32,48,128]{2,1,0:T(8,128)S(1)} %get-tuple-element.21), channel_id=1, replica_groups=mesh['z'=4,'y'=4,'far'=2,'near'=2,'core'=2] {'far','y','z'}, dimensions={0} | all-to-all | bytes 1572864 | tf_op jit(solution)/shard_map/all_to_all | solution.py:410
  58.7 1.3 %opened.1 = f32[3,256,512]{2,1,0:T(8,128)} custom-call(s32[32,48,128]{2,1,0:T(8,128)S(1)} %all_to_all.11.words, f32[8,128]{1,0:T(8,128)S(1)} %get-tuple-element.22.scales), custom_call_target="tpu_custom_call" | custom-call | tf_op jit(solution)/shard_map/opened/pallas_call | solution.py:389
Async XLA Ops:
  5.3 2.8 %collective-permute-start = (s32[3,168,512]{2,1,0:T(8,128)S(1)}, s32[3,168,512]{2,1,0:T(8,128)S(1)}, u32[]{:S(2)}, u32[]{:S(2)}) collective-permute-start(s32[3,168,512]{2,1,0:T(8,128)S(1)} %get-tuple-element.20), channel_id=1, source_target_pairs={{0,1},{1,0},{2,3},{3,2},{4,5},{5,4},{6,7},{7,6},{8,9},{9,8},{10,11... | collective-permute-start | bytes 3096584 | tf_op jit(solution)/shard_map/ppermute | solution.py:404

commit v7 on v6

--- a/solution.py
+++ b/solution.py
@@ -273,20 +273,21 @@
     )(mine, theirs)
 
 
+def device_of(source, x, m):
+    return (m & 1) * HEADS + x * (HEADS // 2) + source + column_of(m)
+
+
+def reached(scale):
+    halves = []
+    for x in range(2):
+        top = scale[x, 0]
+        for m in range(1, GROUP_DEVS):
+            top = jnp.maximum(top, scale[x, m])
+        halves.append(top)
+    return halves[0] + halves[1]
+
+
 def route_kernel(src, grp, slot, words, out, scales, whole_q, where_q):
-    reach = []
-    for x in range(2):
-        tops = []
-        for parity in range(2):
-            top = None
-            for m in range(HEADS // 2):
-                code = high_of(words[parity * HEADS + x * (HEADS // 2) + m, 24:32, :])
-                top = code if top is None else jnp.maximum(top, code)
-            tops.append(top)
-        reach.append(scale_of(jnp.maximum(tops[0], pltpu.roll(tops[1], 64, 1))))
-    reach = reach[0] + reach[1]
-    scales[...] = reach
-    inverse = 1.0 / reach[:, 96:97]
     left = lanes() < 64
 
     @pl.loop(0, KV_HEADS, unroll=True)
@@ -295,6 +296,13 @@
         target = column_of(grp[r] * GROUP_DEVS)
         for j in range(GROUP):
             where_q[slot[r * GROUP + j]] = j
+        scale = {}
+        for x in range(2):
+            for m in range(GROUP_DEVS):
+                code = high_of(words[device_of(source, x, m), 24:32, :])
+                at = 96 if m % 2 == 0 else 32
+                scale[x, m] = scale_of(code[:, at : at + 1])
+        inverse = 1.0 / reached(scale)
         blocks = [[None] * 10 for _ in range(LAYERS)]
         for pair in range(2):
             even, odd = 2 * pair, 2 * pair + 1
@@ -303,11 +311,10 @@
             for x in range(2):
                 third = {}
                 for m in (even, odd):
-                    device = (m & 1) * HEADS + x * (HEADS // 2) + source + column_of(m)
+                    device = device_of(source, x, m)
                     last = words[device, 24:32, :]
                     low, high = low_of(last), high_of(last)
-                    at = 96 if m == even else 32
-                    ratio = scale_of(high[:, at : at + 1]) * inverse
+                    ratio = scale[x, m] * inverse
                     third[m] = (low.astype(jnp.float32) * ratio, high.astype(jnp.float32) * ratio)
                     for l in range(LAYERS):
                         word = words[device, 8 * l : 8 * l + 8, :]
@@ -345,6 +352,19 @@
             for l in range(LAYERS):
                 out[device, 8 * l : 8 * l + 8, :] = packed(whole_q[first, l], whole_q[second, l])
 
+    own = lax.axis_index("z") * 2 + (lax.axis_index("y") >> 1)
+    block = 0
+    for r in range(KV_HEADS):
+        block = jnp.where(grp[r] == own, src[r], block)
+    source = column_of(block * GROUP_DEVS)
+    scale = {}
+    for x in range(2):
+        for m in range(GROUP_DEVS):
+            code = high_of(words[device_of(source, x, m), 24:32, :])
+            code = code if m % 2 == 0 else pltpu.roll(code, 64, 1)
+            scale[x, m] = scale_of(code)
+    scales[...] = reached(scale)
+
 
 def route(src, grp, slot, words):
     return pl.pallas_call(

time: 60.2 us -> 60.3 us (level)
  no operation moved by 1% of the time
where the time goes in v7:
time: 60.3 us; the launch traced here: 60.1 us
  blocking collectives  49.2 us (82%)
  Pallas kernels  10.8 us (18%)
    all_to_all x1, blocking collectives, on_device(): words = lax.all_to_all(words, ('far', 'near', 'y', 'z'), 0, 0, tiled=True)  30.5 us
    all_to_all x1, blocking collectives, on_device(): words = lax.all_to_all(words, ('far', 'y', 'z'), 0, 0, tiled=True)  18.7 us
    pallas_call x1, Pallas kernels, away_product(): pl.pallas_call(away_kernel, in_specs=[HBM, HBM], out_specs=[VMEM, VMEM, V...  5.27 us
    pallas_call x1, Pallas kernels, my_product(): pl.pallas_call(my_kernel, in_specs=[HBM, VMEM, VMEM, HBM, HBM, HBM], out_...  2.72 us
    pallas_call x1, Pallas kernels, opened(): pl.pallas_call(open_kernel, grid=(HEADS // OPEN_HEADS,), in_specs=[VMEM,...  1.33 us
  transfers between devices with their start and end apart: 1, of which 0 were waited for; matrix products, arithmetic and copies ran while one was open for 0% of the time, Pallas kernels for 5%

profile of v7, /device:TPU:0, one launch (start us, length us, event | category | flops | bytes accessed | tf_op | source)
XLA Modules:
  0.0 60.1 jit_solution(13664369299680455403)
XLA Ops:
  0.0 5.3 %away_product.1 = (s32[3,168,512]{2,1,0:T(8,128)S(1)}, bf16[2,512,2048]{2,1,0:T(8,128)(2,1)S(1)}, bf16[3,320,2048]{2,1,0:T(8,128)(2,1)S(1)}) custom-call(bf16[3,1024,2048]{2,1,0:T(8,128)(2,1)} %hidden.3, bf16[3,320,2048]{2,1,0:T(8,128)(2,1)} %bitcast.1), custom_call_target="tpu_custom_call" | custom-call | flops 2013265920 | bytes 20000000 | tf_op jit(solution)/shard_map/away_product/pallas_call | solution.py:131
  5.3 0.1 collective-permute-start
  5.4 2.7 %my_product.1 = (f32[3,320,512]{2,1,0:T(8,128)S(1)}, s32[8]{0:T(128)S(4)}, s32[8]{0:T(128)S(4)}, s32[64]{0:T(128)S(4)}) custom-call(bf16[3,1024,2048]{2,1,0:T(8,128)(2,1)} %hidden.3, bf16[2,512,2048]{2,1,0:T(8,128)(2,1)S(1)} %get-tuple-element.14.rows, bf16[3,320,2048]{2,1,0:T(8,128)(2,1)S(1)} %get-tuple-element.15.weight, s32[8]{0:T(128)} %src.1, s32[8]{0:T(128)} %grp.1, ...), custom_call_target="tpu_custom_call" | custom-call | flops 2013265920 | bytes 12000000 | tf_op jit(solution)/shard_map/my_product/pallas_call | solution.py:181
  8.1 0.0 collective-permute-done.theirs
  8.1 0.9 %pack.1 = s32[64,32,128]{2,1,0:T(8,128)S(1)} custom-call(f32[3,320,512]{2,1,0:T(8,128)S(1)} %get-tuple-element.19.mine, s32[3,168,512]{2,1,0:T(8,128)S(1)} %collective-permute-done.theirs), custom_call_target="tpu_custom_call" | custom-call | tf_op jit(solution)/shard_map/pack/pallas_call | solution.py:265
  9.0 30.5 %all_to_all.10.words = s32[64,32,128]{2,1,0:T(8,128)S(1)} all-to-all(s32[64,32,128]{2,1,0:T(8,128)S(1)} %pack.1), channel_id=1, replica_groups=mesh['z'=4,'y'=4,'far'=2,'near'=2,'core'=2] {'far','near','y','z'}, dimensions={0} | all-to-all | bytes 2097152 | tf_op jit(solution)/shard_map/all_to_all | solution.py:428
  39.5 0.6 %route.1 = (s32[32,48,128]{2,1,0:T(8,128)S(1)}, f32[8,128]{1,0:T(8,128)S(1)}) custom-call(s32[8]{0:T(128)S(4)} %get-tuple-element.16.src, s32[8]{0:T(128)S(4)} %get-tuple-element.17.grp, s32[64]{0:T(128)S(4)} %get-tuple-element.18.slot, s32[64,32,128]{2,1,0:T(8,128)S(1)} %all_to_all.10.words), custom_call_target="tpu_custom_call" | custom-call | tf_op jit(solution)/shard_map/route/pallas_call | solution.py:370
  40.1 18.7 %all_to_all.11.words = s32[32,48,128]{2,1,0:T(8,128)S(1)} all-to-all(s32[32,48,128]{2,1,0:T(8,128)S(1)} %get-tuple-element.21), channel_id=1, replica_groups=mesh['z'=4,'y'=4,'far'=2,'near'=2,'core'=2] {'far','y','z'}, dimensions={0} | all-to-all | bytes 1572864 | tf_op jit(solution)/shard_map/all_to_all | solution.py:430
  58.8 1.3 %opened.1 = f32[3,256,512]{2,1,0:T(8,128)} custom-call(s32[32,48,128]{2,1,0:T(8,128)S(1)} %all_to_all.11.words, f32[8,128]{1,0:T(8,128)S(1)} %get-tuple-element.22.scales), custom_call_target="tpu_custom_call" | custom-call | tf_op jit(solution)/shard_map/opened/pallas_call | solution.py:409
Async XLA Ops:
  5.3 2.8 %collective-permute-start = (s32[3,168,512]{2,1,0:T(8,128)S(1)}, s32[3,168,512]{2,1,0:T(8,128)S(1)}, u32[]{:S(2)}, u32[]{:S(2)}) collective-permute-start(s32[3,168,512]{2,1,0:T(8,128)S(1)} %get-tuple-element.20), channel_id=1, source_target_pairs={{0,1},{1,0},{2,3},{3,2},{4,5},{5,4},{6,7},{7,6},{8,9},{9,8},{10,11... | collective-permute-start | bytes 3096584 | tf_op jit(solution)/shard_map/ppermute | solution.py:424

commit v8 on v7

--- a/solution.py
+++ b/solution.py
@@ -210,7 +210,7 @@
     spare = (lane >= 64) != is_odd
     slot = lane & 63
 
-    @pl.loop(0, 2)
+    @pl.loop(0, 2, unroll=True)
     def _(x):
         codes = jnp.zeros((8, LANES), jnp.int32)
         first = x * (HEADS // 2)

time: 60.3 us -> 60.2 us (level)
  no operation moved by 1% of the time
where the time goes in v8:
time: 60.2 us; the launch traced here: 60 us
  blocking collectives  49.2 us (82%)
  Pallas kernels  10.7 us (18%)
    all_to_all x1, blocking collectives, on_device(): words = lax.all_to_all(words, ('far', 'near', 'y', 'z'), 0, 0, tiled=True)  30.5 us
    all_to_all x1, blocking collectives, on_device(): words = lax.all_to_all(words, ('far', 'y', 'z'), 0, 0, tiled=True)  18.7 us
    pallas_call x1, Pallas kernels, away_product(): pl.pallas_call(away_kernel, in_specs=[HBM, HBM], out_specs=[VMEM, VMEM, V...  5.27 us
    pallas_call x1, Pallas kernels, my_product(): pl.pallas_call(my_kernel, in_specs=[HBM, VMEM, VMEM, HBM, HBM, HBM], out_...  2.72 us
    pallas_call x1, Pallas kernels, opened(): pl.pallas_call(open_kernel, grid=(HEADS // OPEN_HEADS,), in_specs=[VMEM,...  1.33 us
  transfers between devices with their start and end apart: 1, of which 0 were waited for; matrix products, arithmetic and copies ran while one was open for 0% of the time, Pallas kernels for 5%

profile of v8, /device:TPU:0, one launch (start us, length us, event | category | flops | bytes accessed | tf_op | source)
XLA Modules:
  0.0 60.0 jit_solution(8910433758730411966)
XLA Ops:
  0.0 5.3 %away_product.1 = (s32[3,168,512]{2,1,0:T(8,128)S(1)}, bf16[2,512,2048]{2,1,0:T(8,128)(2,1)S(1)}, bf16[3,320,2048]{2,1,0:T(8,128)(2,1)S(1)}) custom-call(bf16[3,1024,2048]{2,1,0:T(8,128)(2,1)} %hidden.3, bf16[3,320,2048]{2,1,0:T(8,128)(2,1)} %bitcast.1), custom_call_target="tpu_custom_call" | custom-call | flops 2013265920 | bytes 20000000 | tf_op jit(solution)/shard_map/away_product/pallas_call | solution.py:131
  5.3 0.1 collective-permute-start
  5.4 2.7 %my_product.1 = (f32[3,320,512]{2,1,0:T(8,128)S(1)}, s32[8]{0:T(128)S(4)}, s32[8]{0:T(128)S(4)}, s32[64]{0:T(128)S(4)}) custom-call(bf16[3,1024,2048]{2,1,0:T(8,128)(2,1)} %hidden.3, bf16[2,512,2048]{2,1,0:T(8,128)(2,1)S(1)} %get-tuple-element.14.rows, bf16[3,320,2048]{2,1,0:T(8,128)(2,1)S(1)} %get-tuple-element.15.weight, s32[8]{0:T(128)} %src.1, s32[8]{0:T(128)} %grp.1, ...), custom_call_target="tpu_custom_call" | custom-call | flops 2013265920 | bytes 12000000 | tf_op jit(solution)/shard_map/my_product/pallas_call | solution.py:181
  8.1 0.0 collective-permute-done.theirs
  8.1 0.7 %pack.1 = s32[64,32,128]{2,1,0:T(8,128)S(1)} custom-call(f32[3,320,512]{2,1,0:T(8,128)S(1)} %get-tuple-element.19.mine, s32[3,168,512]{2,1,0:T(8,128)S(1)} %collective-permute-done.theirs), custom_call_target="tpu_custom_call" | custom-call | tf_op jit(solution)/shard_map/pack/pallas_call | solution.py:265
  8.9 30.5 %all_to_all.10.words = s32[64,32,128]{2,1,0:T(8,128)S(1)} all-to-all(s32[64,32,128]{2,1,0:T(8,128)S(1)} %pack.1), channel_id=1, replica_groups=mesh['z'=4,'y'=4,'far'=2,'near'=2,'core'=2] {'far','near','y','z'}, dimensions={0} | all-to-all | bytes 2097152 | tf_op jit(solution)/shard_map/all_to_all | solution.py:428
  39.4 0.6 %route.1 = (s32[32,48,128]{2,1,0:T(8,128)S(1)}, f32[8,128]{1,0:T(8,128)S(1)}) custom-call(s32[8]{0:T(128)S(4)} %get-tuple-element.16.src, s32[8]{0:T(128)S(4)} %get-tuple-element.17.grp, s32[64]{0:T(128)S(4)} %get-tuple-element.18.slot, s32[64,32,128]{2,1,0:T(8,128)S(1)} %all_to_all.10.words), custom_call_target="tpu_custom_call" | custom-call | tf_op jit(solution)/shard_map/route/pallas_call | solution.py:370
  40.0 18.7 %all_to_all.11.words = s32[32,48,128]{2,1,0:T(8,128)S(1)} all-to-all(s32[32,48,128]{2,1,0:T(8,128)S(1)} %get-tuple-element.21), channel_id=1, replica_groups=mesh['z'=4,'y'=4,'far'=2,'near'=2,'core'=2] {'far','y','z'}, dimensions={0} | all-to-all | bytes 1572864 | tf_op jit(solution)/shard_map/all_to_all | solution.py:430
  58.7 1.3 %opened.1 = f32[3,256,512]{2,1,0:T(8,128)} custom-call(s32[32,48,128]{2,1,0:T(8,128)S(1)} %all_to_all.11.words, f32[8,128]{1,0:T(8,128)S(1)} %get-tuple-element.22.scales), custom_call_target="tpu_custom_call" | custom-call | tf_op jit(solution)/shard_map/opened/pallas_call | solution.py:409
Async XLA Ops:
  5.3 2.8 %collective-permute-start = (s32[3,168,512]{2,1,0:T(8,128)S(1)}, s32[3,168,512]{2,1,0:T(8,128)S(1)}, u32[]{:S(2)}, u32[]{:S(2)}) collective-permute-start(s32[3,168,512]{2,1,0:T(8,128)S(1)} %get-tuple-element.20), channel_id=1, source_target_pairs={{0,1},{1,0},{2,3},{3,2},{4,5},{5,4},{6,7},{7,6},{8,9},{9,8},{10,11... | collective-permute-start | bytes 3096584 | tf_op jit(solution)/shard_map/ppermute | solution.py:424

commit v9 on v8

--- a/solution.py
+++ b/solution.py
@@ -216,7 +216,7 @@
         first = x * (HEADS // 2)
 
         def place(head):
-            return (head & 1) * HEADS + column_of(head)
+            return (head & 1) * HEADS + (head >> 1)
 
         for j in range(SLICE // LANES):
             tokens = pl.ds(pl.multiple_of(x * SLICE + j * LANES, LANES), LANES)
@@ -274,7 +274,7 @@
 
 
 def device_of(source, x, m):
-    return (m & 1) * HEADS + x * (HEADS // 2) + source + column_of(m)
+    return (m & 1) * HEADS + x * (HEADS // 2) + source + (m >> 1)
 
 
 def reached(scale):
@@ -292,7 +292,7 @@
 
     @pl.loop(0, KV_HEADS, unroll=True)
     def _(r):
-        source = column_of(src[r] * GROUP_DEVS)
+        source = src[r] * (GROUP_DEVS // 2)
         target = column_of(grp[r] * GROUP_DEVS)
         for j in range(GROUP):
             where_q[slot[r * GROUP + j]] = j
@@ -356,7 +356,7 @@
     block = 0
     for r in range(KV_HEADS):
         block = jnp.where(grp[r] == own, src[r], block)
-    source = column_of(block * GROUP_DEVS)
+    source = block * (GROUP_DEVS // 2)
     scale = {}
     for x in range(2):
         for m in range(GROUP_DEVS):
@@ -425,7 +425,7 @@
     tables = [pltpu.with_memory_space_constraint(t, pltpu.HBM) for t in (src_block, group_map, q_slot)]
     mine, *tables = my_product(hidden, rows, weight, *tables)
     words = pack(mine, theirs)
-    words = lax.all_to_all(words, ("far", "near", "y", "z"), 0, 0, tiled=True)
+    words = lax.all_to_all(words, ("far", "near", "z", "y"), 0, 0, tiled=True)
     words, scales = route(*tables, words)
     words = lax.all_to_all(words, ("far", "y", "z"), 0, 0, tiled=True)
     return opened(words, scales)

time: 60.2 us -> 60.3 us (level)
  no operation moved by 1% of the time
where the time goes in v9:
time: 60.3 us; the launch traced here: 60.1 us
  blocking collectives  49.3 us (82%)
  Pallas kernels  10.7 us (18%)
    all_to_all x1, blocking collectives, on_device(): words = lax.all_to_all(words, ('far', 'near', 'z', 'y'), 0, 0, tiled=True)  30.5 us
    all_to_all x1, blocking collectives, on_device(): words = lax.all_to_all(words, ('far', 'y', 'z'), 0, 0, tiled=True)  18.8 us
    pallas_call x1, Pallas kernels, away_product(): pl.pallas_call(away_kernel, in_specs=[HBM, HBM], out_specs=[VMEM, VMEM, V...  5.27 us
    pallas_call x1, Pallas kernels, my_product(): pl.pallas_call(my_kernel, in_specs=[HBM, VMEM, VMEM, HBM, HBM, HBM], out_...  2.72 us
    pallas_call x1, Pallas kernels, opened(): pl.pallas_call(open_kernel, grid=(HEADS // OPEN_HEADS,), in_specs=[VMEM,...  1.33 us
  transfers between devices with their start and end apart: 1, of which 0 were waited for; matrix products, arithmetic and copies ran while one was open for 0% of the time, Pallas kernels for 5%

profile of v9, /device:TPU:0, one launch (start us, length us, event | category | flops | bytes accessed | tf_op | source)
XLA Modules:
  0.0 60.1 jit_solution(640200864712217343)
XLA Ops:
  0.0 5.3 %away_product.1 = (s32[3,168,512]{2,1,0:T(8,128)S(1)}, bf16[2,512,2048]{2,1,0:T(8,128)(2,1)S(1)}, bf16[3,320,2048]{2,1,0:T(8,128)(2,1)S(1)}) custom-call(bf16[3,1024,2048]{2,1,0:T(8,128)(2,1)} %hidden.3, bf16[3,320,2048]{2,1,0:T(8,128)(2,1)} %bitcast.1), custom_call_target="tpu_custom_call" | custom-call | flops 2013265920 | bytes 20000000 | tf_op jit(solution)/shard_map/away_product/pallas_call | solution.py:131
  5.3 0.1 collective-permute-start
  5.4 2.7 %my_product.1 = (f32[3,320,512]{2,1,0:T(8,128)S(1)}, s32[8]{0:T(128)S(4)}, s32[8]{0:T(128)S(4)}, s32[64]{0:T(128)S(4)}) custom-call(bf16[3,1024,2048]{2,1,0:T(8,128)(2,1)} %hidden.3, bf16[2,512,2048]{2,1,0:T(8,128)(2,1)S(1)} %get-tuple-element.14.rows, bf16[3,320,2048]{2,1,0:T(8,128)(2,1)S(1)} %get-tuple-element.15.weight, s32[8]{0:T(128)} %src.1, s32[8]{0:T(128)} %grp.1, ...), custom_call_target="tpu_custom_call" | custom-call | flops 2013265920 | bytes 12000000 | tf_op jit(solution)/shard_map/my_product/pallas_call | solution.py:181
  8.1 0.0 collective-permute-done.theirs
  8.1 0.7 %pack.1 = s32[64,32,128]{2,1,0:T(8,128)S(1)} custom-call(f32[3,320,512]{2,1,0:T(8,128)S(1)} %get-tuple-element.19.mine, s32[3,168,512]{2,1,0:T(8,128)S(1)} %collective-permute-done.theirs), custom_call_target="tpu_custom_call" | custom-call | tf_op jit(solution)/shard_map/pack/pallas_call | solution.py:265
  8.9 30.5 %all_to_all.10.words = s32[64,32,128]{2,1,0:T(8,128)S(1)} all-to-all(s32[64,32,128]{2,1,0:T(8,128)S(1)} %pack.1), channel_id=1, replica_groups=mesh['z'=4,'y'=4,'far'=2,'near'=2,'core'=2] {'far','near','z','y'}, dimensions={0} | all-to-all | bytes 2097152 | tf_op jit(solution)/shard_map/all_to_all | solution.py:428
  39.4 0.6 %route.1 = (s32[32,48,128]{2,1,0:T(8,128)S(1)}, f32[8,128]{1,0:T(8,128)S(1)}) custom-call(s32[8]{0:T(128)S(4)} %get-tuple-element.16.src, s32[8]{0:T(128)S(4)} %get-tuple-element.17.grp, s32[64]{0:T(128)S(4)} %get-tuple-element.18.slot, s32[64,32,128]{2,1,0:T(8,128)S(1)} %all_to_all.10.words), custom_call_target="tpu_custom_call" | custom-call | tf_op jit(solution)/shard_map/route/pallas_call | solution.py:370
  40.0 18.8 %all_to_all.11.words = s32[32,48,128]{2,1,0:T(8,128)S(1)} all-to-all(s32[32,48,128]{2,1,0:T(8,128)S(1)} %get-tuple-element.21), channel_id=1, replica_groups=mesh['z'=4,'y'=4,'far'=2,'near'=2,'core'=2] {'far','y','z'}, dimensions={0} | all-to-all | bytes 1572864 | tf_op jit(solution)/shard_map/all_to_all | solution.py:430
  58.8 1.3 %opened.1 = f32[3,256,512]{2,1,0:T(8,128)} custom-call(s32[32,48,128]{2,1,0:T(8,128)S(1)} %all_to_all.11.words, f32[8,128]{1,0:T(8,128)S(1)} %get-tuple-element.22.scales), custom_call_target="tpu_custom_call" | custom-call | tf_op jit(solution)/shard_map/opened/pallas_call | solution.py:409
Async XLA Ops:
  5.3 2.8 %collective-permute-start = (s32[3,168,512]{2,1,0:T(8,128)S(1)}, s32[3,168,512]{2,1,0:T(8,128)S(1)}, u32[]{:S(2)}, u32[]{:S(2)}) collective-permute-start(s32[3,168,512]{2,1,0:T(8,128)S(1)} %get-tuple-element.20), channel_id=1, source_target_pairs={{0,1},{1,0},{2,3},{3,2},{4,5},{5,4},{6,7},{7,6},{8,9},{9,8},{10,11... | collective-permute-start | bytes 3096584 | tf_op jit(solution)/shard_map/ppermute | solution.py:424
